TPU v7x, 32 devices: a whole 2x2x4 slice. The times are simulated.
32 devices in a mesh: group: 4 (over y, core), dev: 8 (over z, x).
Axes of the slice: x: 2, y: 2, z: 4, core: 2. Of those that a mesh axis runs over, the one named last changes fastest.
Arguments:
- points: bfloat16 [8192, 256], P(('group', 'dev')), may hold values from -6 to 6
- base_factor: float32 [8192, 256], P(('group', 'dev')), may hold values from -0.12 to 0.12
- pivots: int32 [2, 64], replicated, may hold values from 0 to 8191, as said below
Outputs:
- new_factor: float32 [8192, 128], P(('group', 'dev'))
- residual_diag: float32 [8192], P(('group', 'dev'))
Inputs may be any that keep to these rules, and one draw needn't show every extreme that they name: `pivots`: all 128 pivot indices are distinct; most of them fall on the points of a few devices.
All inputs are finite; a program needn't handle non-finite values.
Results may differ from a plain program's by a relative error of at most 0.0003.
Values sent between devices are 32-bit elements; how exact they have to be, the bound alone decides.
No kernel may reach another device: no remote copies, remote signals or barrier semaphores. Data moves between devices by JAX's collectives and lax.ppermute only.
A program may use at most 64 MiB of HBM per device.

v0:
```python
import jax
import jax.numpy as jnp
from jax import lax
from jax.sharding import PartitionSpec as P

DIM = 256
PIV = 64
ROUNDS = 2


def kernel_rows(rows, row_norms, centres, centre_norms):
    inner = jnp.dot(rows, centres.T, preferred_element_type=jnp.float32)
    dist = row_norms[:, None] + centre_norms[None, :] - 2.0 * inner
    return jnp.exp(-2.0 * dist / DIM)


def per_device(points, base_factor, pivots):
    local_rows = points.shape[0]
    device = lax.axis_index(("group", "dev"))
    norms = jnp.sum(points.astype(jnp.float32) ** 2, axis=1)
    factor = base_factor
    diag = 1.0 - jnp.sum(base_factor * base_factor, axis=1)
    positions = lax.broadcasted_iota(jnp.int32, (1, local_rows), 1)
    every_offset = pivots.reshape(-1) - device * local_rows
    every_select = (every_offset[:, None] == positions).astype(jnp.float32)
    every_points = jnp.dot(
        every_select.astype(jnp.bfloat16), points, preferred_element_type=jnp.float32
    )
    every_base = jnp.dot(every_select, base_factor, precision=lax.Precision.HIGHEST)
    every_centres, pivot_factor = lax.psum((every_points, every_base), ("group", "dev"))
    every_norms = jnp.sum(every_centres * every_centres, axis=1)
    every_half = every_centres.astype(jnp.bfloat16)
    collected = []
    for step in range(ROUNDS):
        offsets = pivots[step] - device * local_rows
        select = (offsets[:, None] == positions).astype(jnp.float32)
        centres = every_centres[step * PIV : (step + 1) * PIV]
        factor_rows = pivot_factor[step * PIV : (step + 1) * PIV]
        centre_norms = jnp.sum(centres * centres, axis=1)
        centre_half = centres.astype(jnp.bfloat16)
        resid = kernel_rows(points, norms, centre_half, centre_norms) - jnp.dot(
            factor, factor_rows.T, precision=lax.Precision.HIGHEST
        )
        block = lax.psum(jnp.dot(select, resid, precision=lax.Precision.HIGHEST), ("group", "dev"))
        lower = jnp.linalg.cholesky(block)
        inverse = lax.linalg.triangular_solve(
            lower, jnp.eye(block.shape[0], dtype=block.dtype), left_side=True, lower=True
        )
        cols = jnp.dot(resid, inverse.T, precision=lax.Precision.HIGHEST)
        diag = diag - jnp.sum(cols * cols, axis=1)
        factor = jnp.concatenate([factor, cols], axis=1)
        collected.append(cols)
        if step + 1 < ROUNDS:
            pivot_resid = kernel_rows(every_half, every_norms, centre_half, centre_norms) - jnp.dot(
                pivot_factor, factor_rows.T, precision=lax.Precision.HIGHEST
            )
            pivot_cols = jnp.dot(pivot_resid, inverse.T, precision=lax.Precision.HIGHEST)
            pivot_factor = jnp.concatenate([pivot_factor, pivot_cols], axis=1)
    return (jnp.concatenate(collected, axis=1), diag)


def solution(mesh):
    return jax.shard_map(
        per_device,
        mesh=mesh,
        in_specs=(P(("group", "dev"), None), P(("group", "dev"), None), P()),
        out_specs=(P(("group", "dev"), None), P(("group", "dev"))),
        check_vma=False,
    )
```

profile of v0, /device:TPU:0, one launch (start us, length us, event | category | flops | bytes accessed | tf_op | source)
XLA Modules:
  0.0 260.4 jit_solution(3146454910611682736)
XLA Ops:
  7.2 0.0 all-reduce.3.cloned.1.call-start
  7.2 0.0 copy-start.4
  7.2 0.7 copy-done.4
  7.9 0.1 sub.69
  8.0 0.0 copy-start.2
  8.0 1.9 fusion.17
  9.9 0.0 copy-done.2
  9.9 0.9 fusion.19
  10.8 0.0 copy-start
  10.8 0.0 all-reduce.3.cloned.1.call-update
  10.8 0.1 multiply_reduce_fusion.1
  10.9 0.8 copy-done
  11.7 0.1 multiply_reduce_fusion
  11.8 131.9 %all-reduce.3.cloned.1.call-done = (f32[128,256]{1,0:T(8,128)}, f32[128,256]{1,0:T(8,128)}) async-done(((f32[128,256]{1,0:T(8,128)}, f32[128,256]{1,0:T(8,128)}), (f32[128,256]{1,0:T(8,128)}, f32[128,256]{1,0:T(8,128)})) %all-reduce.3.cloned.1.call-update) | async-done | bytes 262160 | tf_op jit(solution)/shard_map/psum | solution.py:30
  143.8 0.0 copy-start.1
  143.8 0.0 copy-start.3
  143.8 1.0 multiply_reduce_fusion.5
  144.8 0.0 copy-done.1
  144.8 0.1 multiply_reduce_fusion.2
  144.9 0.0 copy-done.3
  144.9 0.4 convolution_bitcast_fusion
  145.3 0.2 fusion.9
  145.5 0.2 fusion.23
  145.8 39.4 %psum.30 = f32[64,64]{0,1:T(8,128)S(1)} all-reduce(f32[64,64]{0,1:T(8,128)S(1)} %fusion.23), channel_id=1, replica_groups=mesh['group'=4,'dev'=8] {'group','dev'}, use_global_device_ids=true, to_apply=%region_4.0 | all-reduce | flops 4096 | bytes 32768 | tf_op jit(solution)/shard_map/psum | solution.py:44
  185.2 0.1 copy.6
  185.3 5.8 %cholesky.44 = f32[64,64]{1,0:T(8,128)S(1)} custom-call(f32[64,64]{1,0:T(8,128)S(1)} %fusion.36), custom_call_target="Cholesky" | custom-call | tf_op jit(solution)/shard_map/jit(cholesky)/cholesky | solution.py:45
  191.2 0.6 compare_reduce_fusion.1
  191.8 0.7 fusion.31
  192.5 4.9 %custom-call.6 = f32[1,64,64]{1,2,0:T(8,128)S(1)} custom-call(f32[1,64,64]{2,1,0:T(8,128)S(1)} %fusion.31), custom_call_target="InvertDiagBlocksLowerTriangular" | custom-call | tf_op jit(solution)/shard_map/triangular_solve/custom-call.0 | solution.py:46
  197.4 0.3 fusion.29
  197.6 0.2 fusion.2
  197.8 0.3 convolution_subtract_fusion
  198.1 0.2 multiply_reduce_fusion.4
  198.3 0.2 fusion.40
  198.5 0.1 copy.7
  198.6 0.5 fusion.13
  199.1 0.2 fusion.12
  199.3 0.2 fusion.24
  199.5 40.0 %psum.31 = f32[64,64]{0,1:T(8,128)S(1)} all-reduce(f32[64,64]{0,1:T(8,128)S(1)} %fusion.24), channel_id=1, replica_groups=mesh['group'=4,'dev'=8] {'group','dev'}, use_global_device_ids=true, to_apply=%region_9.12 | all-reduce | flops 4096 | bytes 32768 | tf_op jit(solution)/shard_map/psum | solution.py:44
  239.6 0.1 copy.9
  239.7 5.8 %cholesky.55 = f32[64,64]{1,0:T(8,128)S(1)} custom-call(f32[64,64]{1,0:T(8,128)S(1)} %fusion.34), custom_call_target="Cholesky" | custom-call | tf_op jit(solution)/shard_map/jit(cholesky)/cholesky | solution.py:45
  245.6 0.6 compare_reduce_fusion
  246.2 0.7 fusion.32
  246.9 4.9 %custom-call.7 = f32[1,64,64]{1,2,0:T(8,128)S(1)} custom-call(f32[1,64,64]{2,1,0:T(8,128)S(1)} %fusion.32), custom_call_target="InvertDiagBlocksLowerTriangular" | custom-call | tf_op jit(solution)/shard_map/triangular_solve/custom-call.0 | solution.py:46
  251.8 0.3 fusion.27
  252.0 0.2 multiply_reduce_fusion.3
  252.3 0.8 copy.10
  253.0 0.6 subtract_subtract_fusion
  (7 shorter events, 0.1 us)
Async XLA Ops:
  7.2 136.6 %all-reduce.3.cloned.1.call-start = ((), (), s32[]{:S(2)}) async-start(), calls=%async_computation | async-start | bytes 524288 | tf_op jit(solution)/shard_map/psum | solution.py:30
  7.2 0.7 copy-start.4
  8.0 1.9 copy-start.2
  10.8 0.9 copy-start
  143.8 1.0 copy-start.1
  143.8 1.1 copy-start.3
Sparse Core Ops, SparseCore 0:
  14.2 129.4 all-reduce.2
where the time goes:
time: 261 us; the launch traced here: 260 us
  waiting for transfers between devices  132 us (51%)
  blocking collectives  79.5 us (30%)
  other arithmetic  26.1 us (10%)
  between operations  14.2 us (5%)
  matrix products  6.1 us (2%)
    psum x1, waiting for transfers between devices, per_device(): lax.psum((every_points, every_base), ('group', 'dev'))  132 us
    psum x2, blocking collectives, per_device(): lax.psum(jnp.dot(select, resid, precision=lax.Precision.HIGHEST), ('group...  79.5 us
    another operation x6, other arithmetic, per_device(): lower = jnp.linalg.cholesky(block)  13 us
    another operation x4, other arithmetic, per_device(): lax.linalg.triangular_solve(lower, jnp.eye(block.shape[0], dtype=block.dt...  11.1 us
  transfers between devices with their start and end apart: 1, of which 1 were waited for; matrix products, arithmetic and copies ran while one was open for 0% of the time, Pallas kernels for 0%

commit v1 on v0

v1 whole, which is shorter than its diff:
```python
import functools

import jax
import jax.numpy as jnp
from jax import lax
from jax.experimental import pallas as pl
from jax.experimental.pallas import tpu as pltpu
from jax.sharding import PartitionSpec as P

AXES = ("group", "dev")
BLOCK = 32
HIGHEST = lax.Precision.HIGHEST


def dot_nt(a, b, precision=None):
    return lax.dot_general(a, b, (((1,), (1,)), ((), ())), precision=precision, preferred_element_type=jnp.float32)


def dot_tn(a, b, precision=None):
    return lax.dot_general(a, b, (((0,), (0,)), ((), ())), precision=precision, preferred_element_type=jnp.float32)


def dot_nn(a, b, precision=None):
    return lax.dot_general(a, b, (((1,), (0,)), ((), ())), precision=precision, preferred_element_type=jnp.float32)


def pick_kernel(pivots_ref, points_ref, base_ref, mine_ref, other_ref):
    rows, dim = points_ref.shape
    half = mine_ref.shape[0]
    member = lax.axis_index("group")
    device = member * lax.axis_size("dev") + lax.axis_index("dev")
    core = member % 2
    positions = lax.broadcasted_iota(jnp.int32, (rows, half), 0) + device * rows
    points = points_ref[...]
    base = base_ref[...]
    high = base.astype(jnp.bfloat16)
    rest = base - high.astype(jnp.float32)
    middle = rest.astype(jnp.bfloat16)
    low = (rest - middle.astype(jnp.float32)).astype(jnp.bfloat16)
    for ref, which in ((mine_ref, core), (other_ref, 1 - core)):
        pivots = pivots_ref[pl.ds(which, 1), :]
        chosen = (positions == pivots).astype(jnp.bfloat16)
        ref[:, :dim] = dot_tn(chosen, points)
        ref[:, dim:] = dot_tn(chosen, high) + dot_tn(chosen, middle) + dot_tn(chosen, low)


def factor_kernel(mine_ref, other_ref, points_ref, base_ref, cols_ref, diag_ref, pivot_ref, work_ref):
    half, width = mine_ref.shape
    total = 2 * half
    rows, dim = points_ref.shape
    core = lax.axis_index("group") % 2
    pivot_ref[pl.ds(pl.multiple_of(core * half, half), half), :] = mine_ref[...]
    pivot_ref[pl.ds(pl.multiple_of((1 - core) * half, half), half), :] = other_ref[...]
    points = points_ref[...]
    base = base_ref[...]
    centres = pivot_ref[:, :dim].astype(jnp.bfloat16)
    pivot_base = pivot_ref[:, dim:]

    ones = jnp.ones((8, dim), jnp.float32)
    wide = points.astype(jnp.float32)
    norms = dot_nt(ones, wide * wide, HIGHEST)[0:1, :]
    start = 1.0 - dot_nt(ones, base * base, HIGHEST)[0:1, :]

    gram = dot_nt(centres, centres)
    eye = lax.broadcasted_iota(jnp.int32, (total, total), 0) == lax.broadcasted_iota(jnp.int32, (total, total), 1)
    own = jnp.where(eye, gram, 0.0)
    norm_lane = jnp.sum(own, axis=0, keepdims=True)
    norm_row = jnp.sum(own, axis=1, keepdims=True)
    scale = -2.0 / dim
    schur = jnp.exp(scale * (norm_row + norm_lane - 2.0 * gram)) - dot_nt(pivot_base, pivot_base, HIGHEST)
    inner = dot_nt(centres, points)
    resid = jnp.exp(scale * (norm_row + norms - 2.0 * inner)) - dot_nt(pivot_base, base, HIGHEST)
    work_ref[:, :total] = schur
    work_ref[:, total:] = resid

    b = BLOCK
    row_id = lax.broadcasted_iota(jnp.int32, (8, 128), 0)
    done = []
    for first in range(0, total, b):
        panel = [[work_ref[first + 8 * g : first + 8 * g + 8, 128 * t : 128 * t + 128] for t in range((total + rows) // 128)] for g in range(b // 8)]
        tile, lane0 = first // 128, first % 128
        rep = [
            [jnp.broadcast_to(panel[g][tile][:, lane0 + c : lane0 + c + 1], (8, 128)) if g >= c // 8 else None for g in range(b // 8)]
            for c in range(b)
        ]
        roots = [jnp.zeros((8, 128), jnp.float32) for _ in range(b // 8)]
        for j in range(b):
            gj, sj = j // 8, j % 8
            pivot = jnp.broadcast_to(rep[j][gj][sj : sj + 1, :], (8, 128))
            inverse = 1.0 / pivot
            roots[gj] = jnp.where(row_id == sj, lax.rsqrt(pivot), roots[gj])
            weight = [None] * (b // 8)
            for g in range(gj, b // 8):
                weight[g] = rep[j][g] * inverse
                if g == gj:
                    weight[g] = jnp.where(row_id > sj, weight[g], 0.0)
            for c in range(j + 1, b):
                gc, sc = c // 8, c % 8
                entry = jnp.broadcast_to(rep[j][gc][sc : sc + 1, :], (8, 128))
                for g in range(gc, b // 8):
                    rep[c][g] = rep[c][g] - weight[g] * entry
            for t in range(len(panel[0])):
                if 128 * t + 127 <= first:
                    continue
                line = jnp.broadcast_to(panel[gj][t][sj : sj + 1, :], (8, 128))
                for g in range(gj, b // 8):
                    panel[g][t] = panel[g][t] - weight[g] * line
        upper = jnp.concatenate(
            [jnp.concatenate([panel[g][t] * roots[g] for t in range(len(panel[0]))], axis=1) for g in range(b // 8)], axis=0
        )
        done.append(upper[:, total:])
        after = first + b
        if after < total:
            change = dot_tn(upper[:, :total], upper, HIGHEST)
            work_ref[after:, :] = work_ref[after:, :] - change[after:, :]
    cols = jnp.concatenate(done, axis=0)
    cols_ref[...] = cols.T
    diag_ref[...] = start - jnp.sum(cols * cols, axis=0, keepdims=True)


def exchange(mine, other, mesh):
    groups, devs = mesh.shape["group"], mesh.shape["dev"]
    half, width = mine.shape

    def swap(value, partner):
        return lax.ppermute(value, AXES, [(i, partner(i)) for i in range(groups * devs)])

    total = mine + swap(other, lambda i: i ^ devs)
    step = 1
    while step < devs:
        total = total + swap(total, lambda i: i ^ step)
        step *= 2
    step = 2
    while step < groups:
        total = total + swap(total, lambda i: i ^ (step * devs))
        step *= 2
    return total, swap(total, lambda i: i ^ devs)


def vmem(n):
    return [pl.BlockSpec(memory_space=pltpu.VMEM)] * n


def per_device(points, base_factor, pivots, mesh):
    rows, dim = points.shape
    rounds, half = pivots.shape
    base = base_factor.shape[1]
    piece = jax.ShapeDtypeStruct((half, dim + base), jnp.float32)
    mine, other = pl.pallas_call(
        pick_kernel,
        out_shape=(piece, piece),
        in_specs=vmem(3),
        out_specs=tuple(vmem(2)),
        name="pick",
    )(pivots, points, base_factor)
    mine, other = exchange(mine, other, mesh)
    total = rounds * half
    cols, diag = pl.pallas_call(
        factor_kernel,
        out_shape=(
            jax.ShapeDtypeStruct((rows, total), jnp.float32),
            jax.ShapeDtypeStruct((1, rows), jnp.float32),
        ),
        in_specs=vmem(4),
        out_specs=tuple(vmem(2)),
        scratch_shapes=[
            pltpu.VMEM((total, dim + base), jnp.float32),
            pltpu.VMEM((total, total + rows), jnp.float32),
        ],
        name="factor",
    )(mine, other, points, base_factor)
    return cols, diag.reshape(rows)


def solution(mesh):
    return jax.shard_map(
        functools.partial(per_device, mesh=mesh),
        mesh=mesh,
        in_specs=(P(AXES, None), P(AXES, None), P()),
        out_specs=(P(AXES, None), P(AXES)),
        check_vma=False,
    )
```

time: 261 us -> 39.1 us (0.15)
  waiting for transfers between devices: 132 us -> 18.2 us
  blocking collectives: 79.5 us -> 0 us
  other arithmetic: 26.1 us -> 1 us
  between operations: 14.2 us -> 0.67 us
  starting transfers between devices: 0.04 us -> 9.52 us
  Pallas kernels: 0 us -> 8.87 us
  matrix products: 6.1 us -> 0 us
    psum x1 -> x0, waiting for transfers between devices: 132 us -> none  [per_device(): lax.psum((every_points, every_base), ('group', 'dev'))]
    psum x2 -> x0, blocking collectives: 79.5 us -> none  [per_device(): lax.psum(jnp.dot(select, resid, precision=lax.Precision.HIGHEST), ('group...]
    another operation x10 -> x0, other arithmetic: 24.1 us -> none  [the longest x6 13 us: per_device(): lower = jnp.linalg.cholesky(block)]
    ppermute x0 -> x6, waiting for transfers between devices: none -> 18.2 us  [swap(): lax.ppermute(value, AXES, [(i, partner(i)) for i in range(groups * devs)])]
    ppermute x0 -> x6, starting transfers between devices: none -> 9.52 us  [swap(): lax.ppermute(value, AXES, [(i, partner(i)) for i in range(groups * devs)])]
    pallas_call x0 -> x2, Pallas kernels: none -> 8.87 us  [the longest x1 6.79 us: per_device(): pl.pallas_call(factor_kernel, out_shape=(jax.ShapeDtypeStruct((rows, tota...]
    dot_general x13 -> x0, matrix products: 5.6 us -> none  [the longest x1 1.91 us: per_device(): jnp.dot(every_select, base_factor, precision=lax.Precision.HIGHEST)]
  transfers between devices with their start and end apart: 1 -> 6, of which waited for: 1 -> 6; matrix products, arithmetic and copies ran while one was open for 0% -> 0% of each run, Pallas kernels for 0% -> 0%
where the time goes in v1:
time: 39.1 us; the launch traced here: 39 us
  waiting for transfers between devices  18.2 us (47%)
  starting transfers between devices  9.52 us (24%)
  Pallas kernels  8.87 us (23%)
  other arithmetic  1 us (3%)
  between operations  0.67 us (2%)
  local copies, waits for them, and re-layouts  0.66 us (2%)
    ppermute x6, waiting for transfers between devices, swap(): lax.ppermute(value, AXES, [(i, partner(i)) for i in range(groups * devs)])  18.2 us
    ppermute x6, starting transfers between devices, swap(): lax.ppermute(value, AXES, [(i, partner(i)) for i in range(groups * devs)])  9.52 us
    pallas_call x1, Pallas kernels, per_device(): pl.pallas_call(factor_kernel, out_shape=(jax.ShapeDtypeStruct((rows, tota...  6.79 us
    pallas_call x1, Pallas kernels, per_device(): pl.pallas_call(pick_kernel, out_shape=(piece, piece), in_specs=vmem(3), o...  2.08 us
    add x1, other arithmetic, exchange(): total = mine + swap(other, lambda i: i ^ devs)  0.93 us
  transfers between devices with their start and end apart: 6, of which 6 were waited for; matrix products, arithmetic and copies ran while one was open for 0% of the time, Pallas kernels for 0%

profile of v1, /device:TPU:0, one launch (start us, length us, event | category | flops | bytes accessed | tf_op | source)
XLA Modules:
  0.0 39.0 jit_solution(17491636544324364557)
XLA Ops:
  0.6 2.1 %pick.1 = (f32[64,512]{1,0:T(8,128)}, f32[64,512]{1,0:T(8,128)}) custom-call(s32[2,64]{1,0:T(2,128)} %pivots_ref.1, bf16[256,256]{1,0:T(8,128)(2,1)} %points_ref.3, f32[256,256]{1,0:T(8,128)} %base_ref.3), custom_call_target="tpu_custom_call" | custom-call | tf_op jit(solution)/shard_map/pick/pallas_call | solution.py:149
  2.7 0.5 %collective-permute-start = (f32[64,512]{1,0:T(8,128)}, f32[64,512]{1,0:T(8,128)S(1)}, u32[]{:S(2)}, u32[]{:S(2)}) collective-permute-start(f32[64,512]{1,0:T(8,128)} %get-tuple-element.7), channel_id=1, source_target_pairs={{0,8},{1,9},{2,10},{3,11},{4,12},{5,13},{6,14},{7,15},{8,0},{9,1},... | collective-permute-start | bytes 393224 | tf_op jit(solution)/shard_map/ppermute | solution.py:126
  3.2 1.2 %collective-permute-done = f32[64,512]{1,0:T(8,128)S(1)} collective-permute-done((f32[64,512]{1,0:T(8,128)}, f32[64,512]{1,0:T(8,128)S(1)}, u32[]{:S(2)}, u32[]{:S(2)}) %collective-permute-start) | collective-permute-done | bytes 131104 | tf_op jit(solution)/shard_map/ppermute | solution.py:126
  4.4 0.9 %add.15 = f32[64,512]{1,0:T(8,128)S(1)} add(f32[64,512]{1,0:T(8,128)} %get-tuple-element.6, f32[64,512]{1,0:T(8,128)S(1)} %collective-permute-done) | non-fusion elementwise | flops 32768 | bytes 393216 | tf_op jit(solution)/shard_map/add | solution.py:128
  5.3 2.9 %collective-permute-start.1 = (f32[64,512]{1,0:T(8,128)S(1)}, f32[64,512]{1,0:T(8,128)S(1)}, u32[]{:S(2)}, u32[]{:S(2)}) collective-permute-start(f32[64,512]{1,0:T(8,128)S(1)} %add.15), channel_id=1, source_target_pairs={{0,1},{1,0},{2,3},{3,2},{4,5},{5,4},{6,7},{7,6},{8,9},{9,8},{10,11... | collective-permute-start | bytes 393224 | tf_op jit(solution)/shard_map/ppermute | solution.py:126
  8.2 3.8 %collective-permute-done.1 = f32[64,512]{1,0:T(8,128)S(1)} collective-permute-done((f32[64,512]{1,0:T(8,128)S(1)}, f32[64,512]{1,0:T(8,128)S(1)}, u32[]{:S(2)}, u32[]{:S(2)}) %collective-permute-start.1) | collective-permute-done | bytes 131104 | tf_op jit(solution)/shard_map/ppermute | solution.py:126
  12.1 1.9 %collective-permute-start.2 = (f32[64,512]{1,0:T(8,128)S(1)}, f32[64,512]{1,0:T(8,128)S(1)}, u32[]{:S(2)}, u32[]{:S(2)}) collective-permute-start(f32[64,512]{1,0:T(8,128)S(1)} %add.16), channel_id=1, source_target_pairs={{0,2},{1,3},{2,0},{3,1},{4,6},{5,7},{6,4},{7,5},{8,10},{9,11},{10,... | collective-permute-start | bytes 393224 | tf_op jit(solution)/shard_map/ppermute | solution.py:126
  14.0 3.1 %collective-permute-done.2 = f32[64,512]{1,0:T(8,128)S(1)} collective-permute-done((f32[64,512]{1,0:T(8,128)S(1)}, f32[64,512]{1,0:T(8,128)S(1)}, u32[]{:S(2)}, u32[]{:S(2)}) %collective-permute-start.2) | collective-permute-done | bytes 131104 | tf_op jit(solution)/shard_map/ppermute | solution.py:126
  17.1 2.9 %collective-permute-start.3 = (f32[64,512]{1,0:T(8,128)S(1)}, f32[64,512]{1,0:T(8,128)S(1)}, u32[]{:S(2)}, u32[]{:S(2)}) collective-permute-start(f32[64,512]{1,0:T(8,128)S(1)} %add.17), channel_id=1, source_target_pairs={{0,4},{1,5},{2,6},{3,7},{4,0},{5,1},{6,2},{7,3},{8,12},{9,13},{10,... | collective-permute-start | bytes 393224 | tf_op jit(solution)/shard_map/ppermute | solution.py:126
  20.0 5.0 %collective-permute-done.3 = f32[64,512]{1,0:T(8,128)S(1)} collective-permute-done((f32[64,512]{1,0:T(8,128)S(1)}, f32[64,512]{1,0:T(8,128)S(1)}, u32[]{:S(2)}, u32[]{:S(2)}) %collective-permute-start.3) | collective-permute-done | bytes 131104 | tf_op jit(solution)/shard_map/ppermute | solution.py:126
  25.0 1.3 %collective-permute-start.4 = (f32[64,512]{1,0:T(8,128)S(1)}, f32[64,512]{1,0:T(8,128)S(1)}, u32[]{:S(2)}, u32[]{:S(2)}) collective-permute-start(f32[64,512]{1,0:T(8,128)S(1)} %add.18), channel_id=1, source_target_pairs={{0,16},{1,17},{2,18},{3,19},{4,20},{5,21},{6,22},{7,23},{8,24},{9,... | collective-permute-start | bytes 393224 | tf_op jit(solution)/shard_map/ppermute | solution.py:126
  26.3 3.8 %collective-permute-done.4 = f32[64,512]{1,0:T(8,128)S(1)} collective-permute-done((f32[64,512]{1,0:T(8,128)S(1)}, f32[64,512]{1,0:T(8,128)S(1)}, u32[]{:S(2)}, u32[]{:S(2)}) %collective-permute-start.4) | collective-permute-done | bytes 131104 | tf_op jit(solution)/shard_map/ppermute | solution.py:126
  30.1 0.0 copy-start
  30.1 0.1 collective-permute-start.5
  30.2 1.3 %collective-permute-done.5.other_ref = f32[64,512]{1,0:T(8,128)S(1)} collective-permute-done((f32[64,512]{1,0:T(8,128)S(1)}, f32[64,512]{1,0:T(8,128)S(1)}, u32[]{:S(2)}, u32[]{:S(2)}) %collective-permute-start.5) | collective-permute-done | bytes 131104 | tf_op jit(solution)/shard_map/ppermute | solution.py:126
  31.5 0.0 copy-done
  31.5 0.0 copy-start.1
  31.5 0.7 %copy-done.1 = f32[64,512]{1,0:T(8,128)} copy-done((f32[64,512]{1,0:T(8,128)}, f32[64,512]{1,0:T(8,128)S(1)}, u32[]{:S(2)}) %copy-start.1) | copy-done | bytes 131096
  32.2 6.8 %factor.1 = (f32[256,128]{1,0:T(8,128)}, f32[1,256]{1,0:T(1,128)}) custom-call(f32[64,512]{1,0:T(8,128)} %copy-done, f32[64,512]{1,0:T(8,128)} %copy-done.1, bf16[256,256]{1,0:T(8,128)(2,1)} %points_ref.3, f32[256,256]{1,0:T(8,128)} %base_ref.3), custom_call_target="tpu_custom_call" | custom-call | tf_op jit(solution)/shard_map/factor/pallas_call | solution.py:158
  (4 shorter events, 0.1 us)
Async XLA Ops:
  2.7 1.7 %collective-permute-start = (f32[64,512]{1,0:T(8,128)}, f32[64,512]{1,0:T(8,128)S(1)}, u32[]{:S(2)}, u32[]{:S(2)}) collective-permute-start(f32[64,512]{1,0:T(8,128)} %get-tuple-element.7), channel_id=1, source_target_pairs={{0,8},{1,9},{2,10},{3,11},{4,12},{5,13},{6,14},{7,15},{8,0},{9,1},... | collective-permute-start | bytes 393224 | tf_op jit(solution)/shard_map/ppermute | solution.py:126
  5.3 6.7 %collective-permute-start.1 = (f32[64,512]{1,0:T(8,128)S(1)}, f32[64,512]{1,0:T(8,128)S(1)}, u32[]{:S(2)}, u32[]{:S(2)}) collective-permute-start(f32[64,512]{1,0:T(8,128)S(1)} %add.15), channel_id=1, source_target_pairs={{0,1},{1,0},{2,3},{3,2},{4,5},{5,4},{6,7},{7,6},{8,9},{9,8},{10,11... | collective-permute-start | bytes 393224 | tf_op jit(solution)/shard_map/ppermute | solution.py:126
  12.1 5.0 %collective-permute-start.2 = (f32[64,512]{1,0:T(8,128)S(1)}, f32[64,512]{1,0:T(8,128)S(1)}, u32[]{:S(2)}, u32[]{:S(2)}) collective-permute-start(f32[64,512]{1,0:T(8,128)S(1)} %add.16), channel_id=1, source_target_pairs={{0,2},{1,3},{2,0},{3,1},{4,6},{5,7},{6,4},{7,5},{8,10},{9,11},{10,... | collective-permute-start | bytes 393224 | tf_op jit(solution)/shard_map/ppermute | solution.py:126
  17.1 7.9 %collective-permute-start.3 = (f32[64,512]{1,0:T(8,128)S(1)}, f32[64,512]{1,0:T(8,128)S(1)}, u32[]{:S(2)}, u32[]{:S(2)}) collective-permute-start(f32[64,512]{1,0:T(8,128)S(1)} %add.17), channel_id=1, source_target_pairs={{0,4},{1,5},{2,6},{3,7},{4,0},{5,1},{6,2},{7,3},{8,12},{9,13},{10,... | collective-permute-start | bytes 393224 | tf_op jit(solution)/shard_map/ppermute | solution.py:126
  25.0 5.0 %collective-permute-start.4 = (f32[64,512]{1,0:T(8,128)S(1)}, f32[64,512]{1,0:T(8,128)S(1)}, u32[]{:S(2)}, u32[]{:S(2)}) collective-permute-start(f32[64,512]{1,0:T(8,128)S(1)} %add.18), channel_id=1, source_target_pairs={{0,16},{1,17},{2,18},{3,19},{4,20},{5,21},{6,22},{7,23},{8,24},{9,... | collective-permute-start | bytes 393224 | tf_op jit(solution)/shard_map/ppermute | solution.py:126
  30.1 1.4 %copy-start = (f32[64,512]{1,0:T(8,128)}, f32[64,512]{1,0:T(8,128)S(1)}, u32[]{:S(2)}) copy-start(f32[64,512]{1,0:T(8,128)S(1)} %add.19.mine_ref) | copy-start | bytes 393220
  30.1 1.4 %collective-permute-start.5 = (f32[64,512]{1,0:T(8,128)S(1)}, f32[64,512]{1,0:T(8,128)S(1)}, u32[]{:S(2)}, u32[]{:S(2)}) collective-permute-start(f32[64,512]{1,0:T(8,128)S(1)} %add.19.mine_ref), channel_id=1, source_target_pairs={{0,8},{1,9},{2,10},{3,11},{4,12},{5,13},{6,14},{7,15},{8,0},{9,1},... | collective-permute-start | bytes 393224 | tf_op jit(solution)/shard_map/ppermute | solution.py:126
  31.5 0.7 %copy-start.1 = (f32[64,512]{1,0:T(8,128)}, f32[64,512]{1,0:T(8,128)S(1)}, u32[]{:S(2)}) copy-start(f32[64,512]{1,0:T(8,128)S(1)} %collective-permute-done.5.other_ref) | copy-start | bytes 393220

commit v2 on v0

v2 whole, which is shorter than its diff:
```python
import functools

import jax
import jax.numpy as jnp
from jax import lax
from jax.experimental import pallas as pl
from jax.experimental.pallas import tpu as pltpu
from jax.sharding import PartitionSpec as P

AXES = ("group", "dev")
WINDOW = 5


def pick_kernel(pivots_ref, points_hbm, base_hbm, *refs):
    outs, (points_ref, base_ref, sems) = refs[:-3], refs[-3:]
    copies = [pltpu.make_async_copy(points_hbm, points_ref, sems.at[0]), pltpu.make_async_copy(base_hbm, base_ref, sems.at[1])]
    for copy in copies:
        copy.start()
    rows, dim = points_ref.shape
    rounds, slots = pivots_ref.shape
    part = slots // 2
    device = lax.axis_index("group") * lax.axis_size("dev") + lax.axis_index("dev")
    first = lax.axis_index("group") % 2 == 0
    start = device * rows
    row_id = lax.broadcasted_iota(jnp.int32, (8, rows), 0)
    lane = lax.broadcasted_iota(jnp.int32, (8, rows), 1)
    chosen = []
    for r in range(rounds):
        groups = []
        for g in range(0, slots, 8):
            index = jnp.full((8, rows), pivots_ref[r, g] - start, jnp.int32)
            for k in range(1, 8):
                index = jnp.where(row_id == k, pivots_ref[r, g + k] - start, index)
            groups.append((index == lane).astype(jnp.float32))
        chosen.append(jnp.concatenate(groups, axis=0).astype(jnp.bfloat16))
    copies[0].wait()
    points = points_ref[...]
    for r in range(rounds):
        rows_of = dot(chosen[r], points, (1, 0))
        outs[2 * r][:, :dim] = jnp.where(first, rows_of[:part], rows_of[part:])
        outs[2 * r + 1][:, :dim] = jnp.where(first, rows_of[part:], rows_of[:part])
    copies[1].wait()
    high, middle, low = split(base_ref[...])
    for r in range(rounds):
        rows_of = sum(dot(chosen[r], x, (1, 0)) for x in (high, middle, low))
        outs[2 * r][:, dim:] = jnp.where(first, rows_of[:part], rows_of[part:])
        outs[2 * r + 1][:, dim:] = jnp.where(first, rows_of[part:], rows_of[:part])


def dot(a, b, dims):
    return lax.dot_general(a, b, ((dims[:1], dims[1:]), ((), ())), preferred_element_type=jnp.float32)

def split(value):
    high = value.astype(jnp.bfloat16)
    rest = value - high.astype(jnp.float32)
    middle = rest.astype(jnp.bfloat16)
    low = (rest - middle.astype(jnp.float32)).astype(jnp.bfloat16)
    return high, middle, low

def product_nt(a, b):
    n = a[0].shape[0]
    first = dot(jnp.concatenate(a, axis=0), b[0], (1, 1))
    second = dot(jnp.concatenate(a[:2], axis=0), b[1], (1, 1))
    third = dot(a[0], b[2], (1, 1))
    return first[:n] + (first[n:2*n] + second[:n]) + (first[2*n:] + second[n:] + third)

def gram_tn(upper, split_at):
    h, m, l = split(upper)
    left = jnp.concatenate([x[:, :split_at] for x in (h, m, h, l, m, h)], axis=0)
    right = jnp.concatenate([h, h, m, h, m, l], axis=0)
    return dot(left, right, (0, 0))

def spread(tile, sub):
    return jnp.broadcast_to(tile[sub:sub + 1, :], (8, 128))

def eliminate(panel, lane0):
    groups, tiles = len(panel), len(panel[0])
    b = 8 * groups
    row_id = lax.broadcasted_iota(jnp.int32, (8, 128), 0)

    def column(c):
        lane = lane0 + c
        return [jnp.broadcast_to(panel[g][0][:, lane:lane + 1], (8, 128)) if g >= c // 8 else None for g in range(groups)]

    rep = {c: column(c) for c in range(min(WINDOW + 1, b))}
    roots = [jnp.zeros((8, 128), jnp.float32) for _ in range(groups)]
    for j in range(b):
        gj, sj = j // 8, j % 8
        mine = rep.pop(j)
        pivot = spread(mine[gj], sj)
        inverse = 1.0 / pivot
        roots[gj] = jnp.where(row_id == sj, lax.rsqrt(pivot), roots[gj])
        weight = [None if g < gj else mine[g] * inverse for g in range(groups)]
        weight[gj] = jnp.where(row_id > sj, weight[gj], 0.0)
        for c in range(j + 1, min(j + WINDOW + 1, b)):
            entry = spread(mine[c // 8], c % 8)
            for g in range(c // 8, groups):
                rep[c][g] = rep[c][g] - weight[g] * entry
        for t in range(tiles):
            line = spread(panel[gj][t], sj)
            for g in range(gj, groups):
                panel[g][t] = panel[g][t] - weight[g] * line
        if j + WINDOW + 1 < b:
            rep[j + WINDOW + 1] = column(j + WINDOW + 1)
    return [[panel[g][t] * roots[g] for t in range(tiles)] for g in range(groups)]

def join(tiles):
    return jnp.concatenate([jnp.concatenate(row, axis=1) for row in tiles], axis=0)

def tiles_of(ref, row, count, tile0, tiles):
    return [[ref[row + 8 * g:row + 8 * g + 8, 128 * t:128 * t + 128] for t in range(tile0, tiles)] for g in range(count // 8)]

def factor_kernel(*refs):
    parts, (points_ref, base_ref, cols_ref, diag_ref, pivot_ref, work_ref) = refs[:-6], refs[-6:]
    part = parts[0].shape[0]
    total = part * len(parts)
    rows, dim = points_ref.shape
    core = lax.axis_index("group") % 2
    for i in range(0, len(parts), 2):
        pivot_ref[pl.ds(pl.multiple_of((i + core) * part, part), part), :] = parts[i][...]
        pivot_ref[pl.ds(pl.multiple_of((i + 1 - core) * part, part), part), :] = parts[i + 1][...]
    points = points_ref[...]
    base = base_ref[...]
    centres = pivot_ref[:, :dim].astype(jnp.bfloat16)
    pivot_base = split(pivot_ref[:, dim:])
    ones = jnp.ones((8, dim), jnp.bfloat16)
    wide = points.astype(jnp.float32)
    base_parts = split(base)
    norms = sum(dot(ones, x, (1, 1)) for x in split(wide * wide))[0:1, :]
    start = 1.0 - sum(dot(ones, x, (1, 1)) for x in split(base * base))[0:1, :]
    gram = dot(centres, centres, (1, 1))
    eye = lax.broadcasted_iota(jnp.int32, (total, total), 0) == lax.broadcasted_iota(jnp.int32, (total, total), 1)
    own = jnp.where(eye, gram, 0.0)
    norm_lane = jnp.sum(own, axis=0, keepdims=True)
    norm_row = jnp.sum(own, axis=1, keepdims=True)
    scale = -2.0 / dim
    work_ref[:, :total] = jnp.exp(scale * (norm_row + norm_lane - 2.0 * gram)) - product_nt(pivot_base, pivot_base)
    inner = dot(centres, points, (1, 1))
    work_ref[:, total:] = jnp.exp(scale * (norm_row + norms - 2.0 * inner)) - product_nt(pivot_base, base_parts)
    half = total // 2
    count = (total + rows) // 128
    top = join(eliminate(tiles_of(work_ref, 0, half, 0, count), 0))
    work_ref[half:, :] = work_ref[half:, :] - gram_tn(top, total)[half:, :]
    bottom = join(eliminate(tiles_of(work_ref, half, half, 0, count), half))
    cols = jnp.concatenate([top[:, total:], bottom[:, total:]], axis=0)
    cols_ref[...] = cols.T
    diag_ref[...] = start - jnp.sum(cols * cols, axis=0, keepdims=True)


def exchange(chains, mesh):
    groups, devs = mesh.shape["group"], mesh.shape["dev"]

    def swap(value, partner):
        return lax.ppermute(value, AXES, [(i, partner(i)) for i in range(groups * devs)])

    def add(a, b):
        return a + b

    near = [1 << k for k in range(devs.bit_length() - 1)]
    far = [devs << k for k in range(1, groups.bit_length() - 1)]
    assert 1 << len(near) == devs and 2 << len(far) == groups
    steps = near[:1] + far + near[1:]
    turn = len(steps) // 2
    orders = (steps, steps[turn:] + steps[:turn])
    got = [swap(chains[2 * r + 1], lambda i: i ^ devs) for r in range(2)]
    sums = [add(chains[2 * r], got[r]) for r in range(2)]
    for k in range(len(steps)):
        got = [swap(sums[r], lambda i: i ^ orders[r][k]) for r in range(2)]
        sums = [add(sums[r], got[r]) for r in range(2)]
    k = len(steps) + 1
    got = [swap(sums[r], lambda i: i ^ devs) for r in range(2)]
    return sums[0], got[0], sums[1], got[1]


def vmem(n):
    return [pl.BlockSpec(memory_space=pltpu.VMEM)] * n


def per_device(points, base_factor, pivots, mesh):
    rows, dim = points.shape
    rounds, slots = pivots.shape
    base = base_factor.shape[1]
    piece = jax.ShapeDtypeStruct((slots // 2, dim + base), jnp.float32)
    n = 2 * rounds
    chains = pl.pallas_call(
        pick_kernel,
        out_shape=(piece,) * n,
        in_specs=[pl.BlockSpec(memory_space=pltpu.SMEM)] + [pl.BlockSpec(memory_space=pl.ANY)] * 2,
        out_specs=tuple(vmem(n)),
        scratch_shapes=[
            pltpu.VMEM(points.shape, points.dtype),
            pltpu.VMEM(base_factor.shape, base_factor.dtype),
            pltpu.SemaphoreType.DMA((2,)),
        ],
        compiler_params=pltpu.CompilerParams(vmem_limit_bytes=54900 * 1024),
        name="pick",
    )(pivots, points, base_factor)
    parts = exchange(chains, mesh)
    total = rounds * slots
    cols, diag = pl.pallas_call(
        factor_kernel,
        out_shape=(
            jax.ShapeDtypeStruct((rows, total), jnp.float32),
            jax.ShapeDtypeStruct((1, rows), jnp.float32),
        ),
        in_specs=vmem(n + 2),
        out_specs=tuple(vmem(2)),
        scratch_shapes=[
            pltpu.VMEM((total, dim + base), jnp.float32),
            pltpu.VMEM((total, total + rows), jnp.float32),
        ],
        compiler_params=pltpu.CompilerParams(vmem_limit_bytes=16 * 2**20),
        name="factor",
    )(*parts, points, base_factor)
    return cols, diag.reshape(rows)


def solution(mesh):
    return jax.shard_map(
        functools.partial(per_device, mesh=mesh),
        mesh=mesh,
        in_specs=(P(AXES, None), P(AXES, None), P()),
        out_specs=(P(AXES, None), P(AXES)),
        check_vma=False,
    )
```

time: 261 us -> 31.6 us (0.12)
  waiting for transfers between devices: 132 us -> 6.28 us
  blocking collectives: 79.5 us -> 0 us
  other arithmetic: 26.1 us -> 0.11 us
  starting transfers between devices: 0.04 us -> 17.7 us
  between operations: 14.2 us -> 0.73 us
  matrix products: 6.1 us -> 0 us
  Pallas kernels: 0 us -> 5.94 us
    psum x1 -> x0, waiting for transfers between devices: 132 us -> none  [per_device(): lax.psum((every_points, every_base), ('group', 'dev'))]
    psum x2 -> x0, blocking collectives: 79.5 us -> none  [per_device(): lax.psum(jnp.dot(select, resid, precision=lax.Precision.HIGHEST), ('group...]
    another operation x10 -> x0, other arithmetic: 24.1 us -> none  [the longest x6 13 us: per_device(): lower = jnp.linalg.cholesky(block)]
    ppermute x0 -> x12, starting transfers between devices: none -> 17.7 us  [swap(): lax.ppermute(value, AXES, [(i, partner(i)) for i in range(groups * devs)])]
    ppermute x0 -> x12, waiting for transfers between devices: none -> 6.28 us  [swap(): lax.ppermute(value, AXES, [(i, partner(i)) for i in range(groups * devs)])]
    pallas_call x0 -> x2, Pallas kernels: none -> 5.94 us  [the longest x1 4.02 us: per_device(): pl.pallas_call(factor_kernel, out_shape=(jax.ShapeDtypeStruct((rows, tota...]
    dot_general x13 -> x0, matrix products: 5.6 us -> none  [the longest x1 1.91 us: per_device(): jnp.dot(every_select, base_factor, precision=lax.Precision.HIGHEST)]
  transfers between devices with their start and end apart: 1 -> 12, of which waited for: 1 -> 7; matrix products, arithmetic and copies ran while one was open for 0% -> 0% of each run, Pallas kernels for 0% -> 0%
where the time goes in v2:
time: 31.6 us; the launch traced here: 31.5 us
  starting transfers between devices  17.7 us (56%)
  waiting for transfers between devices  6.28 us (20%)
  Pallas kernels  5.94 us (19%)
  between operations  0.73 us (2%)
  local copies, waits for them, and re-layouts  0.68 us (2%)
    ppermute x12, starting transfers between devices, swap(): lax.ppermute(value, AXES, [(i, partner(i)) for i in range(groups * devs)])  17.7 us
    ppermute x12, waiting for transfers between devices, swap(): lax.ppermute(value, AXES, [(i, partner(i)) for i in range(groups * devs)])  6.28 us
    pallas_call x1, Pallas kernels, per_device(): pl.pallas_call(factor_kernel, out_shape=(jax.ShapeDtypeStruct((rows, tota...  4.02 us
    pallas_call x1, Pallas kernels, per_device(): pl.pallas_call(pick_kernel, out_shape=(piece,) * n, in_specs=[pl.BlockSpe...  1.92 us
    unnamed x6, local copies, waits for them, and re-layouts  0.68 us
  transfers between devices with their start and end apart: 12, of which 7 were waited for; matrix products, arithmetic and copies ran while one was open for 0% of the time, Pallas kernels for 0%

profile of v2, /device:TPU:0, one launch (start us, length us, event | category | flops | bytes accessed | tf_op | source)
XLA Modules:
  0.0 31.5 jit_solution(14448652096788404426)
XLA Ops:
  0.6 0.0 copy-start.2
  0.6 0.7 %copy-done.2 = s32[2,64]{1,0:T(2,128)S(1)} copy-done((s32[2,64]{1,0:T(2,128)S(1)}, s32[2,64]{1,0:T(2,128)}, u32[]{:S(2)}) %copy-start.2) | copy-done | bytes 536
  1.3 1.9 %pick.1 = (f32[32,512]{1,0:T(8,128)S(1)}, f32[32,512]{1,0:T(8,128)S(1)}, f32[32,512]{1,0:T(8,128)S(1)}, f32[32,512]{1,0:T(8,128)S(1)}) custom-call(s32[2,64]{1,0:T(2,128)S(1)} %copy-done.2, bf16[256,256]{1,0:T(8,128)(2,1)} %refs_4_.1, f32[256,256]{1,0:T(8,128)} %refs_5_.1), custom_call_target="tpu_custom_call" | custom-call | tf_op jit(solution)/shard_map/pick/pallas_call | solution.py:185
  3.2 0.6 %collective-permute-start = (f32[32,512]{1,0:T(8,128)S(1)}, f32[32,512]{1,0:T(8,128)S(1)}, u32[]{:S(2)}, u32[]{:S(2)}) collective-permute-start(f32[32,512]{1,0:T(8,128)S(1)} %get-tuple-element.9), channel_id=1, source_target_pairs={{0,8},{1,9},{2,10},{3,11},{4,12},{5,13},{6,14},{7,15},{8,0},{9,1},... | collective-permute-start | bytes 196616 | tf_op jit(solution)/shard_map/ppermute | solution.py:154
  3.8 0.1 collective-permute-start.6
  3.9 0.8 %collective-permute-done = f32[32,512]{1,0:T(8,128)S(1)} collective-permute-done((f32[32,512]{1,0:T(8,128)S(1)}, f32[32,512]{1,0:T(8,128)S(1)}, u32[]{:S(2)}, u32[]{:S(2)}) %collective-permute-start) | collective-permute-done | bytes 65568 | tf_op jit(solution)/shard_map/ppermute | solution.py:154
  4.7 2.9 %collective-permute-start.1 = (f32[32,512]{1,0:T(8,128)S(1)}, f32[32,512]{1,0:T(8,128)S(1)}, u32[]{:S(2)}, u32[]{:S(2)}) collective-permute-start(f32[32,512]{1,0:T(8,128)S(1)} %add.30), channel_id=1, source_target_pairs={{0,1},{1,0},{2,3},{3,2},{4,5},{5,4},{6,7},{7,6},{8,9},{9,8},{10,11... | collective-permute-start | bytes 196616 | tf_op jit(solution)/shard_map/ppermute | solution.py:154
  7.6 0.0 collective-permute-done.6
  7.6 1.6 %collective-permute-start.7 = (f32[32,512]{1,0:T(8,128)S(1)}, f32[32,512]{1,0:T(8,128)S(1)}, u32[]{:S(2)}, u32[]{:S(2)}) collective-permute-start(f32[32,512]{1,0:T(8,128)S(1)} %add.35), channel_id=1, source_target_pairs={{0,2},{1,3},{2,0},{3,1},{4,6},{5,7},{6,4},{7,5},{8,10},{9,11},{10,... | collective-permute-start | bytes 196616 | tf_op jit(solution)/shard_map/ppermute | solution.py:154
  9.3 0.8 %collective-permute-done.1 = f32[32,512]{1,0:T(8,128)S(1)} collective-permute-done((f32[32,512]{1,0:T(8,128)S(1)}, f32[32,512]{1,0:T(8,128)S(1)}, u32[]{:S(2)}, u32[]{:S(2)}) %collective-permute-start.1) | collective-permute-done | bytes 65568 | tf_op jit(solution)/shard_map/ppermute | solution.py:154
  10.0 1.9 %collective-permute-start.2 = (f32[32,512]{1,0:T(8,128)S(1)}, f32[32,512]{1,0:T(8,128)S(1)}, u32[]{:S(2)}, u32[]{:S(2)}) collective-permute-start(f32[32,512]{1,0:T(8,128)S(1)} %add.31), channel_id=1, source_target_pairs={{0,16},{1,17},{2,18},{3,19},{4,20},{5,21},{6,22},{7,23},{8,24},{9,... | collective-permute-start | bytes 196616 | tf_op jit(solution)/shard_map/ppermute | solution.py:154
  12.0 0.0 collective-permute-done.7
  12.0 2.7 %collective-permute-start.8 = (f32[32,512]{1,0:T(8,128)S(1)}, f32[32,512]{1,0:T(8,128)S(1)}, u32[]{:S(2)}, u32[]{:S(2)}) collective-permute-start(f32[32,512]{1,0:T(8,128)S(1)} %add.36), channel_id=1, source_target_pairs={{0,4},{1,5},{2,6},{3,7},{4,0},{5,1},{6,2},{7,3},{8,12},{9,13},{10,... | collective-permute-start | bytes 196616 | tf_op jit(solution)/shard_map/ppermute | solution.py:154
  14.6 0.0 collective-permute-done.2
  14.7 1.7 %collective-permute-start.3 = (f32[32,512]{1,0:T(8,128)S(1)}, f32[32,512]{1,0:T(8,128)S(1)}, u32[]{:S(2)}, u32[]{:S(2)}) collective-permute-start(f32[32,512]{1,0:T(8,128)S(1)} %add.32), channel_id=1, source_target_pairs={{0,2},{1,3},{2,0},{3,1},{4,6},{5,7},{6,4},{7,5},{8,10},{9,11},{10,... | collective-permute-start | bytes 196616 | tf_op jit(solution)/shard_map/ppermute | solution.py:154
  16.4 0.8 %collective-permute-done.8 = f32[32,512]{1,0:T(8,128)S(1)} collective-permute-done((f32[32,512]{1,0:T(8,128)S(1)}, f32[32,512]{1,0:T(8,128)S(1)}, u32[]{:S(2)}, u32[]{:S(2)}) %collective-permute-start.8) | collective-permute-done | bytes 65568 | tf_op jit(solution)/shard_map/ppermute | solution.py:154
  17.2 1.6 %collective-permute-start.9 = (f32[32,512]{1,0:T(8,128)S(1)}, f32[32,512]{1,0:T(8,128)S(1)}, u32[]{:S(2)}, u32[]{:S(2)}) collective-permute-start(f32[32,512]{1,0:T(8,128)S(1)} %add.37), channel_id=1, source_target_pairs={{0,1},{1,0},{2,3},{3,2},{4,5},{5,4},{6,7},{7,6},{8,9},{9,8},{10,11... | collective-permute-start | bytes 196616 | tf_op jit(solution)/shard_map/ppermute | solution.py:154
  18.8 0.2 collective-permute-done.3
  19.0 0.0 copy-start
  19.0 2.7 %collective-permute-start.4 = (f32[32,512]{1,0:T(8,128)S(1)}, f32[32,512]{1,0:T(8,128)S(1)}, u32[]{:S(2)}, u32[]{:S(2)}) collective-permute-start(f32[32,512]{1,0:T(8,128)S(1)} %add.33), channel_id=1, source_target_pairs={{0,4},{1,5},{2,6},{3,7},{4,0},{5,1},{6,2},{7,3},{8,12},{9,13},{10,... | collective-permute-start | bytes 196616 | tf_op jit(solution)/shard_map/ppermute | solution.py:154
  21.7 0.0 collective-permute-done.9
  21.8 1.8 %collective-permute-start.10 = (f32[32,512]{1,0:T(8,128)S(1)}, f32[32,512]{1,0:T(8,128)S(1)}, u32[]{:S(2)}, u32[]{:S(2)}) collective-permute-start(f32[32,512]{1,0:T(8,128)S(1)} %add.38), channel_id=1, source_target_pairs={{0,16},{1,17},{2,18},{3,19},{4,20},{5,21},{6,22},{7,23},{8,24},{9,... | collective-permute-start | bytes 196616 | tf_op jit(solution)/shard_map/ppermute | solution.py:154
  23.6 0.7 %collective-permute-done.4 = f32[32,512]{1,0:T(8,128)S(1)} collective-permute-done((f32[32,512]{1,0:T(8,128)S(1)}, f32[32,512]{1,0:T(8,128)S(1)}, u32[]{:S(2)}, u32[]{:S(2)}) %collective-permute-start.4) | collective-permute-done | bytes 65568 | tf_op jit(solution)/shard_map/ppermute | solution.py:154
  24.3 0.0 copy-start.1
  24.3 0.1 collective-permute-start.5
  24.4 1.7 %collective-permute-done.10 = f32[32,512]{1,0:T(8,128)S(1)} collective-permute-done((f32[32,512]{1,0:T(8,128)S(1)}, f32[32,512]{1,0:T(8,128)S(1)}, u32[]{:S(2)}, u32[]{:S(2)}) %collective-permute-start.10) | collective-permute-done | bytes 65568 | tf_op jit(solution)/shard_map/ppermute | solution.py:154
  26.1 0.1 collective-permute-start.11
  26.2 0.0 collective-permute-done.5.refs_1_
  26.2 1.2 %collective-permute-done.11.refs_3_ = f32[32,512]{1,0:T(8,128)S(1)} collective-permute-done((f32[32,512]{1,0:T(8,128)S(1)}, f32[32,512]{1,0:T(8,128)S(1)}, u32[]{:S(2)}, u32[]{:S(2)}) %collective-permute-start.11) | collective-permute-done | bytes 65568 | tf_op jit(solution)/shard_map/ppermute | solution.py:154
  27.4 0.0 copy-done
  27.4 0.0 copy-done.1
  27.4 4.0 %factor.1 = (f32[256,128]{1,0:T(8,128)}, f32[1,256]{1,0:T(1,128)}) custom-call(f32[32,512]{1,0:T(8,128)S(1)} %add.34.refs_0_, f32[32,512]{1,0:T(8,128)S(1)} %collective-permute-done.5.refs_1_, f32[32,512]{1,0:T(8,128)S(1)} %add.39.refs_2_, f32[32,512]{1,0:T(8,128)S(1)} %collective-permute-done.11.refs_3_, bf16[256,256]{1,0:T(8,128)(2,1)S(1)} %copy-done.1, ...), custom_call_target="tpu_custom_call" | custom-call | tf_op jit(solution)/shard_map/factor/pallas_call | solution.py:200
  (10 shorter events, 0.1 us)
Async XLA Ops:
  0.6 0.7 %copy-start.2 = (s32[2,64]{1,0:T(2,128)S(1)}, s32[2,64]{1,0:T(2,128)}, u32[]{:S(2)}) copy-start(s32[2,64]{1,0:T(2,128)} %pivots_ref.1) | copy-start | bytes 1540
  3.2 1.5 %collective-permute-start = (f32[32,512]{1,0:T(8,128)S(1)}, f32[32,512]{1,0:T(8,128)S(1)}, u32[]{:S(2)}, u32[]{:S(2)}) collective-permute-start(f32[32,512]{1,0:T(8,128)S(1)} %get-tuple-element.9), channel_id=1, source_target_pairs={{0,8},{1,9},{2,10},{3,11},{4,12},{5,13},{6,14},{7,15},{8,0},{9,1},... | collective-permute-start | bytes 196616 | tf_op jit(solution)/shard_map/ppermute | solution.py:154
  3.8 3.8 %collective-permute-start.6 = (f32[32,512]{1,0:T(8,128)S(1)}, f32[32,512]{1,0:T(8,128)S(1)}, u32[]{:S(2)}, u32[]{:S(2)}) collective-permute-start(f32[32,512]{1,0:T(8,128)S(1)} %get-tuple-element.11), channel_id=1, source_target_pairs={{0,8},{1,9},{2,10},{3,11},{4,12},{5,13},{6,14},{7,15},{8,0},{9,1},... | collective-permute-start | bytes 196616 | tf_op jit(solution)/shard_map/ppermute | solution.py:154
  4.7 5.3 %collective-permute-start.1 = (f32[32,512]{1,0:T(8,128)S(1)}, f32[32,512]{1,0:T(8,128)S(1)}, u32[]{:S(2)}, u32[]{:S(2)}) collective-permute-start(f32[32,512]{1,0:T(8,128)S(1)} %add.30), channel_id=1, source_target_pairs={{0,1},{1,0},{2,3},{3,2},{4,5},{5,4},{6,7},{7,6},{8,9},{9,8},{10,11... | collective-permute-start | bytes 196616 | tf_op jit(solution)/shard_map/ppermute | solution.py:154
  7.6 4.4 %collective-permute-start.7 = (f32[32,512]{1,0:T(8,128)S(1)}, f32[32,512]{1,0:T(8,128)S(1)}, u32[]{:S(2)}, u32[]{:S(2)}) collective-permute-start(f32[32,512]{1,0:T(8,128)S(1)} %add.35), channel_id=1, source_target_pairs={{0,2},{1,3},{2,0},{3,1},{4,6},{5,7},{6,4},{7,5},{8,10},{9,11},{10,... | collective-permute-start | bytes 196616 | tf_op jit(solution)/shard_map/ppermute | solution.py:154
  10.0 4.6 %collective-permute-start.2 = (f32[32,512]{1,0:T(8,128)S(1)}, f32[32,512]{1,0:T(8,128)S(1)}, u32[]{:S(2)}, u32[]{:S(2)}) collective-permute-start(f32[32,512]{1,0:T(8,128)S(1)} %add.31), channel_id=1, source_target_pairs={{0,16},{1,17},{2,18},{3,19},{4,20},{5,21},{6,22},{7,23},{8,24},{9,... | collective-permute-start | bytes 196616 | tf_op jit(solution)/shard_map/ppermute | solution.py:154
  12.0 5.2 %collective-permute-start.8 = (f32[32,512]{1,0:T(8,128)S(1)}, f32[32,512]{1,0:T(8,128)S(1)}, u32[]{:S(2)}, u32[]{:S(2)}) collective-permute-start(f32[32,512]{1,0:T(8,128)S(1)} %add.36), channel_id=1, source_target_pairs={{0,4},{1,5},{2,6},{3,7},{4,0},{5,1},{6,2},{7,3},{8,12},{9,13},{10,... | collective-permute-start | bytes 196616 | tf_op jit(solution)/shard_map/ppermute | solution.py:154
  14.7 4.3 %collective-permute-start.3 = (f32[32,512]{1,0:T(8,128)S(1)}, f32[32,512]{1,0:T(8,128)S(1)}, u32[]{:S(2)}, u32[]{:S(2)}) collective-permute-start(f32[32,512]{1,0:T(8,128)S(1)} %add.32), channel_id=1, source_target_pairs={{0,2},{1,3},{2,0},{3,1},{4,6},{5,7},{6,4},{7,5},{8,10},{9,11},{10,... | collective-permute-start | bytes 196616 | tf_op jit(solution)/shard_map/ppermute | solution.py:154
  17.2 4.5 %collective-permute-start.9 = (f32[32,512]{1,0:T(8,128)S(1)}, f32[32,512]{1,0:T(8,128)S(1)}, u32[]{:S(2)}, u32[]{:S(2)}) collective-permute-start(f32[32,512]{1,0:T(8,128)S(1)} %add.37), channel_id=1, source_target_pairs={{0,1},{1,0},{2,3},{3,2},{4,5},{5,4},{6,7},{7,6},{8,9},{9,8},{10,11... | collective-permute-start | bytes 196616 | tf_op jit(solution)/shard_map/ppermute | solution.py:154
  19.0 8.4 %copy-start = (f32[256,256]{1,0:T(8,128)S(1)}, f32[256,256]{1,0:T(8,128)}, u32[]{:S(2)}) copy-start(f32[256,256]{1,0:T(8,128)} %refs_5_.1) | copy-start | bytes 786436
  19.0 5.2 %collective-permute-start.4 = (f32[32,512]{1,0:T(8,128)S(1)}, f32[32,512]{1,0:T(8,128)S(1)}, u32[]{:S(2)}, u32[]{:S(2)}) collective-permute-start(f32[32,512]{1,0:T(8,128)S(1)} %add.33), channel_id=1, source_target_pairs={{0,4},{1,5},{2,6},{3,7},{4,0},{5,1},{6,2},{7,3},{8,12},{9,13},{10,... | collective-permute-start | bytes 196616 | tf_op jit(solution)/shard_map/ppermute | solution.py:154
  21.8 4.3 %collective-permute-start.10 = (f32[32,512]{1,0:T(8,128)S(1)}, f32[32,512]{1,0:T(8,128)S(1)}, u32[]{:S(2)}, u32[]{:S(2)}) collective-permute-start(f32[32,512]{1,0:T(8,128)S(1)} %add.38), channel_id=1, source_target_pairs={{0,16},{1,17},{2,18},{3,19},{4,20},{5,21},{6,22},{7,23},{8,24},{9,... | collective-permute-start | bytes 196616 | tf_op jit(solution)/shard_map/ppermute | solution.py:154
  24.3 3.2 %copy-start.1 = (bf16[256,256]{1,0:T(8,128)(2,1)S(1)}, bf16[256,256]{1,0:T(8,128)(2,1)}, u32[]{:S(2)}) copy-start(bf16[256,256]{1,0:T(8,128)(2,1)} %refs_4_.1) | copy-start | bytes 393220
  24.3 1.9 %collective-permute-start.5 = (f32[32,512]{1,0:T(8,128)S(1)}, f32[32,512]{1,0:T(8,128)S(1)}, u32[]{:S(2)}, u32[]{:S(2)}) collective-permute-start(f32[32,512]{1,0:T(8,128)S(1)} %add.34.refs_0_), channel_id=1, source_target_pairs={{0,8},{1,9},{2,10},{3,11},{4,12},{5,13},{6,14},{7,15},{8,0},{9,1},... | collective-permute-start | bytes 196616 | tf_op jit(solution)/shard_map/ppermute | solution.py:154
  26.1 1.3 %collective-permute-start.11 = (f32[32,512]{1,0:T(8,128)S(1)}, f32[32,512]{1,0:T(8,128)S(1)}, u32[]{:S(2)}, u32[]{:S(2)}) collective-permute-start(f32[32,512]{1,0:T(8,128)S(1)} %add.39.refs_2_), channel_id=1, source_target_pairs={{0,8},{1,9},{2,10},{3,11},{4,12},{5,13},{6,14},{7,15},{8,0},{9,1},... | collective-permute-start | bytes 196616 | tf_op jit(solution)/shard_map/ppermute | solution.py:154

commit v3 on v2

--- a/solution.py
+++ b/solution.py
@@ -12,7 +12,8 @@
 
 
 def pick_kernel(pivots_ref, points_hbm, base_hbm, *refs):
-    outs, (points_ref, base_ref, sems) = refs[:-3], refs[-3:]
+    outs, local, (base_ref, sems) = refs[:-8], refs[-8:-2], refs[-2:]
+    points_ref, high_ref, middle_ref, low_ref, norms_ref, start_ref = local
     copies = [pltpu.make_async_copy(points_hbm, points_ref, sems.at[0]), pltpu.make_async_copy(base_hbm, base_ref, sems.at[1])]
     for copy in copies:
         copy.start()
@@ -21,30 +22,27 @@
     part = slots // 2
     device = lax.axis_index("group") * lax.axis_size("dev") + lax.axis_index("dev")
     first = lax.axis_index("group") % 2 == 0
-    start = device * rows
-    row_id = lax.broadcasted_iota(jnp.int32, (8, rows), 0)
-    lane = lax.broadcasted_iota(jnp.int32, (8, rows), 1)
-    chosen = []
-    for r in range(rounds):
-        groups = []
-        for g in range(0, slots, 8):
-            index = jnp.full((8, rows), pivots_ref[r, g] - start, jnp.int32)
-            for k in range(1, 8):
-                index = jnp.where(row_id == k, pivots_ref[r, g + k] - start, index)
-            groups.append((index == lane).astype(jnp.float32))
-        chosen.append(jnp.concatenate(groups, axis=0).astype(jnp.bfloat16))
+    positions = lax.broadcasted_iota(jnp.int32, (rows, slots), 0) + device * rows
+    chosen = [(positions == pivots_ref[r : r + 1, :]).astype(jnp.bfloat16) for r in range(rounds)]
+    ones = jnp.ones((8, dim), jnp.bfloat16)
+
+    def put(lanes, pieces):
+        for r in range(rounds):
+            rows_of = sum(dot(chosen[r], piece, (0, 0)) for piece in pieces)
+            outs[2 * r][:, lanes] = jnp.where(first, rows_of[:part], rows_of[part:])
+            outs[2 * r + 1][:, lanes] = jnp.where(first, rows_of[part:], rows_of[:part])
+
     copies[0].wait()
     points = points_ref[...]
-    for r in range(rounds):
-        rows_of = dot(chosen[r], points, (1, 0))
-        outs[2 * r][:, :dim] = jnp.where(first, rows_of[:part], rows_of[part:])
-        outs[2 * r + 1][:, :dim] = jnp.where(first, rows_of[part:], rows_of[:part])
+    put(slice(0, dim), (points,))
+    wide = points.astype(jnp.float32)
+    norms_ref[...] = sum(dot(ones, x, (1, 1)) for x in split(wide * wide)[:2])[0:1, :]
     copies[1].wait()
-    high, middle, low = split(base_ref[...])
-    for r in range(rounds):
-        rows_of = sum(dot(chosen[r], x, (1, 0)) for x in (high, middle, low))
-        outs[2 * r][:, dim:] = jnp.where(first, rows_of[:part], rows_of[part:])
-        outs[2 * r + 1][:, dim:] = jnp.where(first, rows_of[part:], rows_of[:part])
+    base = base_ref[...]
+    parts = split(base)
+    put(slice(dim, None), parts)
+    high_ref[...], middle_ref[...], low_ref[...] = parts
+    start_ref[...] = 1.0 - sum(dot(ones, x, (1, 1)) for x in split(base * base))[0:1, :]
 
 
 def dot(a, b, dims):
@@ -111,7 +109,8 @@
     return [[ref[row + 8 * g:row + 8 * g + 8, 128 * t:128 * t + 128] for t in range(tile0, tiles)] for g in range(count // 8)]
 
 def factor_kernel(*refs):
-    parts, (points_ref, base_ref, cols_ref, diag_ref, pivot_ref, work_ref) = refs[:-6], refs[-6:]
+    parts, local, (cols_ref, diag_ref, pivot_ref, work_ref) = refs[:-10], refs[-10:-4], refs[-4:]
+    points_ref, high_ref, middle_ref, low_ref, norms_ref, start_ref = local
     part = parts[0].shape[0]
     total = part * len(parts)
     rows, dim = points_ref.shape
@@ -120,14 +119,10 @@
         pivot_ref[pl.ds(pl.multiple_of((i + core) * part, part), part), :] = parts[i][...]
         pivot_ref[pl.ds(pl.multiple_of((i + 1 - core) * part, part), part), :] = parts[i + 1][...]
     points = points_ref[...]
-    base = base_ref[...]
+    base_parts = high_ref[...], middle_ref[...], low_ref[...]
+    norms = norms_ref[...]
     centres = pivot_ref[:, :dim].astype(jnp.bfloat16)
     pivot_base = split(pivot_ref[:, dim:])
-    ones = jnp.ones((8, dim), jnp.bfloat16)
-    wide = points.astype(jnp.float32)
-    base_parts = split(base)
-    norms = sum(dot(ones, x, (1, 1)) for x in split(wide * wide))[0:1, :]
-    start = 1.0 - sum(dot(ones, x, (1, 1)) for x in split(base * base))[0:1, :]
     gram = dot(centres, centres, (1, 1))
     eye = lax.broadcasted_iota(jnp.int32, (total, total), 0) == lax.broadcasted_iota(jnp.int32, (total, total), 1)
     own = jnp.where(eye, gram, 0.0)
@@ -144,7 +139,7 @@
     bottom = join(eliminate(tiles_of(work_ref, half, half, 0, count), half))
     cols = jnp.concatenate([top[:, total:], bottom[:, total:]], axis=0)
     cols_ref[...] = cols.T
-    diag_ref[...] = start - jnp.sum(cols * cols, axis=0, keepdims=True)
+    diag_ref[...] = start_ref[...] - jnp.sum(cols * cols, axis=0, keepdims=True)
 
 
 def exchange(chains, mesh):
@@ -184,17 +179,17 @@
     n = 2 * rounds
     chains = pl.pallas_call(
         pick_kernel,
-        out_shape=(piece,) * n,
-        in_specs=[pl.BlockSpec(memory_space=pltpu.SMEM)] + [pl.BlockSpec(memory_space=pl.ANY)] * 2,
-        out_specs=tuple(vmem(n)),
-        scratch_shapes=[
-            pltpu.VMEM(points.shape, points.dtype),
-            pltpu.VMEM(base_factor.shape, base_factor.dtype),
-            pltpu.SemaphoreType.DMA((2,)),
-        ],
-        compiler_params=pltpu.CompilerParams(vmem_limit_bytes=54900 * 1024),
+        out_shape=(piece,) * n
+        + (jax.ShapeDtypeStruct(points.shape, points.dtype),)
+        + (jax.ShapeDtypeStruct(base_factor.shape, jnp.bfloat16),) * 3
+        + (jax.ShapeDtypeStruct((1, rows), jnp.float32),) * 2,
+        in_specs=vmem(1) + [pl.BlockSpec(memory_space=pl.ANY)] * 2,
+        out_specs=tuple(vmem(n + 6)),
+        scratch_shapes=[pltpu.VMEM(base_factor.shape, base_factor.dtype), pltpu.SemaphoreType.DMA((2,))],
+        compiler_params=pltpu.CompilerParams(vmem_limit_bytes=54380 * 1024),
         name="pick",
     )(pivots, points, base_factor)
+    chains, local = chains[:n], chains[n:]
     parts = exchange(chains, mesh)
     total = rounds * slots
     cols, diag = pl.pallas_call(
@@ -203,7 +198,7 @@
             jax.ShapeDtypeStruct((rows, total), jnp.float32),
             jax.ShapeDtypeStruct((1, rows), jnp.float32),
         ),
-        in_specs=vmem(n + 2),
+        in_specs=vmem(n + 6),
         out_specs=tuple(vmem(2)),
         scratch_shapes=[
             pltpu.VMEM((total, dim + base), jnp.float32),
@@ -211,7 +206,7 @@
         ],
         compiler_params=pltpu.CompilerParams(vmem_limit_bytes=16 * 2**20),
         name="factor",
-    )(*parts, points, base_factor)
+    )(*parts, *local)
     return cols, diag.reshape(rows)
 
 

time: 31.6 us -> 31.1 us (0.984)
  Pallas kernels: 5.94 us -> 5.48 us
    unnamed x6 -> x2, local copies, waits for them, and re-layouts: 0.68 us -> 0.67 us
where the time goes in v3:
time: 31.1 us; the launch traced here: 31 us
  starting transfers between devices  17.7 us (57%)
  waiting for transfers between devices  6.28 us (20%)
  Pallas kernels  5.48 us (18%)
  between operations  0.71 us (2%)
  local copies, waits for them, and re-layouts  0.67 us (2%)
    ppermute x12, starting transfers between devices, swap(): lax.ppermute(value, AXES, [(i, partner(i)) for i in range(groups * devs)])  17.7 us
    ppermute x12, waiting for transfers between devices, swap(): lax.ppermute(value, AXES, [(i, partner(i)) for i in range(groups * devs)])  6.28 us
    pallas_call x1, Pallas kernels, per_device(): pl.pallas_call(factor_kernel, out_shape=(jax.ShapeDtypeStruct((rows, tota...  3.81 us
    pallas_call x1, Pallas kernels, per_device(): pl.pallas_call(pick_kernel, out_shape=(piece,) * n + (jax.ShapeDtypeStruc...  1.67 us
    unnamed x2, local copies, waits for them, and re-layouts  0.67 us
  transfers between devices with their start and end apart: 12, of which 7 were waited for; matrix products, arithmetic and copies ran while one was open for 0% of the time, Pallas kernels for 0%

profile of v3, /device:TPU:0, one launch (start us, length us, event | category | flops | bytes accessed | tf_op | source)
XLA Modules:
  0.0 31.0 jit_solution(16461211355936841531)
XLA Ops:
  0.6 0.0 copy-start
  0.6 0.7 %copy-done = s32[2,64]{1,0:T(2,128)S(1)} copy-done((s32[2,64]{1,0:T(2,128)S(1)}, s32[2,64]{1,0:T(2,128)}, u32[]{:S(2)}) %copy-start) | copy-done | bytes 536
  1.3 1.7 %pick.1 = (f32[32,512]{1,0:T(8,128)S(1)}, f32[32,512]{1,0:T(8,128)S(1)}, f32[32,512]{1,0:T(8,128)S(1)}, f32[32,512]{1,0:T(8,128)S(1)}, bf16[256,256]{1,0:T(8,128...) custom-call(s32[2,64]{1,0:T(2,128)S(1)} %copy-done, ...), custom_call_target="tpu_custom_call" | custom-call | tf_op jit(solution)/shard_map/pick/pallas_call | solution.py:180
  3.0 0.6 %collective-permute-start = (f32[32,512]{1,0:T(8,128)S(1)}, f32[32,512]{1,0:T(8,128)S(1)}, u32[]{:S(2)}, u32[]{:S(2)}) collective-permute-start(f32[32,512]{1,0:T(8,128)S(1)} %get-tuple-element.15), channel_id=1, source_target_pairs={{0,8},{1,9},{2,10},{3,11},{4,12},{5,13},{6,14},{7,15},{8,0},{9,1},... | collective-permute-start | bytes 196616 | tf_op jit(solution)/shard_map/ppermute | solution.py:149
  3.5 0.1 collective-permute-start.6
  3.6 0.8 %collective-permute-done = f32[32,512]{1,0:T(8,128)S(1)} collective-permute-done((f32[32,512]{1,0:T(8,128)S(1)}, f32[32,512]{1,0:T(8,128)S(1)}, u32[]{:S(2)}, u32[]{:S(2)}) %collective-permute-start) | collective-permute-done | bytes 65568 | tf_op jit(solution)/shard_map/ppermute | solution.py:149
  4.5 2.9 %collective-permute-start.1 = (f32[32,512]{1,0:T(8,128)S(1)}, f32[32,512]{1,0:T(8,128)S(1)}, u32[]{:S(2)}, u32[]{:S(2)}) collective-permute-start(f32[32,512]{1,0:T(8,128)S(1)} %add.30), channel_id=1, source_target_pairs={{0,1},{1,0},{2,3},{3,2},{4,5},{5,4},{6,7},{7,6},{8,9},{9,8},{10,11... | collective-permute-start | bytes 196616 | tf_op jit(solution)/shard_map/ppermute | solution.py:149
  7.4 0.0 collective-permute-done.6
  7.4 1.6 %collective-permute-start.7 = (f32[32,512]{1,0:T(8,128)S(1)}, f32[32,512]{1,0:T(8,128)S(1)}, u32[]{:S(2)}, u32[]{:S(2)}) collective-permute-start(f32[32,512]{1,0:T(8,128)S(1)} %add.35), channel_id=1, source_target_pairs={{0,2},{1,3},{2,0},{3,1},{4,6},{5,7},{6,4},{7,5},{8,10},{9,11},{10,... | collective-permute-start | bytes 196616 | tf_op jit(solution)/shard_map/ppermute | solution.py:149
  9.0 0.8 %collective-permute-done.1 = f32[32,512]{1,0:T(8,128)S(1)} collective-permute-done((f32[32,512]{1,0:T(8,128)S(1)}, f32[32,512]{1,0:T(8,128)S(1)}, u32[]{:S(2)}, u32[]{:S(2)}) %collective-permute-start.1) | collective-permute-done | bytes 65568 | tf_op jit(solution)/shard_map/ppermute | solution.py:149
  9.8 1.9 %collective-permute-start.2 = (f32[32,512]{1,0:T(8,128)S(1)}, f32[32,512]{1,0:T(8,128)S(1)}, u32[]{:S(2)}, u32[]{:S(2)}) collective-permute-start(f32[32,512]{1,0:T(8,128)S(1)} %add.31), channel_id=1, source_target_pairs={{0,16},{1,17},{2,18},{3,19},{4,20},{5,21},{6,22},{7,23},{8,24},{9,... | collective-permute-start | bytes 196616 | tf_op jit(solution)/shard_map/ppermute | solution.py:149
  11.7 0.0 collective-permute-done.7
  11.7 2.7 %collective-permute-start.8 = (f32[32,512]{1,0:T(8,128)S(1)}, f32[32,512]{1,0:T(8,128)S(1)}, u32[]{:S(2)}, u32[]{:S(2)}) collective-permute-start(f32[32,512]{1,0:T(8,128)S(1)} %add.36), channel_id=1, source_target_pairs={{0,4},{1,5},{2,6},{3,7},{4,0},{5,1},{6,2},{7,3},{8,12},{9,13},{10,... | collective-permute-start | bytes 196616 | tf_op jit(solution)/shard_map/ppermute | solution.py:149
  14.4 0.0 collective-permute-done.2
  14.4 1.7 %collective-permute-start.3 = (f32[32,512]{1,0:T(8,128)S(1)}, f32[32,512]{1,0:T(8,128)S(1)}, u32[]{:S(2)}, u32[]{:S(2)}) collective-permute-start(f32[32,512]{1,0:T(8,128)S(1)} %add.32), channel_id=1, source_target_pairs={{0,2},{1,3},{2,0},{3,1},{4,6},{5,7},{6,4},{7,5},{8,10},{9,11},{10,... | collective-permute-start | bytes 196616 | tf_op jit(solution)/shard_map/ppermute | solution.py:149
  16.1 0.8 %collective-permute-done.8 = f32[32,512]{1,0:T(8,128)S(1)} collective-permute-done((f32[32,512]{1,0:T(8,128)S(1)}, f32[32,512]{1,0:T(8,128)S(1)}, u32[]{:S(2)}, u32[]{:S(2)}) %collective-permute-start.8) | collective-permute-done | bytes 65568 | tf_op jit(solution)/shard_map/ppermute | solution.py:149
  17.0 1.6 %collective-permute-start.9 = (f32[32,512]{1,0:T(8,128)S(1)}, f32[32,512]{1,0:T(8,128)S(1)}, u32[]{:S(2)}, u32[]{:S(2)}) collective-permute-start(f32[32,512]{1,0:T(8,128)S(1)} %add.37), channel_id=1, source_target_pairs={{0,1},{1,0},{2,3},{3,2},{4,5},{5,4},{6,7},{7,6},{8,9},{9,8},{10,11... | collective-permute-start | bytes 196616 | tf_op jit(solution)/shard_map/ppermute | solution.py:149
  18.5 0.2 collective-permute-done.3
  18.8 2.7 %collective-permute-start.4 = (f32[32,512]{1,0:T(8,128)S(1)}, f32[32,512]{1,0:T(8,128)S(1)}, u32[]{:S(2)}, u32[]{:S(2)}) collective-permute-start(f32[32,512]{1,0:T(8,128)S(1)} %add.33), channel_id=1, source_target_pairs={{0,4},{1,5},{2,6},{3,7},{4,0},{5,1},{6,2},{7,3},{8,12},{9,13},{10,... | collective-permute-start | bytes 196616 | tf_op jit(solution)/shard_map/ppermute | solution.py:149
  21.5 0.0 collective-permute-done.9
  21.5 1.8 %collective-permute-start.10 = (f32[32,512]{1,0:T(8,128)S(1)}, f32[32,512]{1,0:T(8,128)S(1)}, u32[]{:S(2)}, u32[]{:S(2)}) collective-permute-start(f32[32,512]{1,0:T(8,128)S(1)} %add.38), channel_id=1, source_target_pairs={{0,16},{1,17},{2,18},{3,19},{4,20},{5,21},{6,22},{7,23},{8,24},{9,... | collective-permute-start | bytes 196616 | tf_op jit(solution)/shard_map/ppermute | solution.py:149
  23.3 0.7 %collective-permute-done.4 = f32[32,512]{1,0:T(8,128)S(1)} collective-permute-done((f32[32,512]{1,0:T(8,128)S(1)}, f32[32,512]{1,0:T(8,128)S(1)}, u32[]{:S(2)}, u32[]{:S(2)}) %collective-permute-start.4) | collective-permute-done | bytes 65568 | tf_op jit(solution)/shard_map/ppermute | solution.py:149
  24.0 0.1 collective-permute-start.5
  24.1 1.8 %collective-permute-done.10 = f32[32,512]{1,0:T(8,128)S(1)} collective-permute-done((f32[32,512]{1,0:T(8,128)S(1)}, f32[32,512]{1,0:T(8,128)S(1)}, u32[]{:S(2)}, u32[]{:S(2)}) %collective-permute-start.10) | collective-permute-done | bytes 65568 | tf_op jit(solution)/shard_map/ppermute | solution.py:149
  25.9 0.1 collective-permute-start.11
  25.9 0.0 collective-permute-done.5.refs_1_
  25.9 1.2 %collective-permute-done.11.refs_3_ = f32[32,512]{1,0:T(8,128)S(1)} collective-permute-done((f32[32,512]{1,0:T(8,128)S(1)}, f32[32,512]{1,0:T(8,128)S(1)}, u32[]{:S(2)}, u32[]{:S(2)}) %collective-permute-start.11) | collective-permute-done | bytes 65568 | tf_op jit(solution)/shard_map/ppermute | solution.py:149
  27.2 3.8 %factor.1 = (f32[256,128]{1,0:T(8,128)}, f32[1,256]{1,0:T(1,128)}) custom-call(f32[32,512]{1,0:T(8,128)S(1)} %add.34.refs_0_, f32[32,512]{1,0:T(8,128)S(1)} %collective-permute-done.5.refs_1_, f32[32,512]{1,0:T(8,128)S(1)} %add.39.refs_2_, f32[32,512]{1,0:T(8,128)S(1)} %collective-permute-done.11.refs_3_, bf16[256,256]{1,0:T(8,128)(2,1)S(1)} %get-tuple-element.18.refs_4_, ...), custom_call_target="tpu_custom_call" | custom-call | tf_op jit(solution)/shard_map/factor/pallas_call | solution.py:195
  (10 shorter events, 0.1 us)
Async XLA Ops:
  0.6 0.7 %copy-start = (s32[2,64]{1,0:T(2,128)S(1)}, s32[2,64]{1,0:T(2,128)}, u32[]{:S(2)}) copy-start(s32[2,64]{1,0:T(2,128)} %pivots_ref.1) | copy-start | bytes 1540
  3.0 1.5 %collective-permute-start = (f32[32,512]{1,0:T(8,128)S(1)}, f32[32,512]{1,0:T(8,128)S(1)}, u32[]{:S(2)}, u32[]{:S(2)}) collective-permute-start(f32[32,512]{1,0:T(8,128)S(1)} %get-tuple-element.15), channel_id=1, source_target_pairs={{0,8},{1,9},{2,10},{3,11},{4,12},{5,13},{6,14},{7,15},{8,0},{9,1},... | collective-permute-start | bytes 196616 | tf_op jit(solution)/shard_map/ppermute | solution.py:149
  3.5 3.8 %collective-permute-start.6 = (f32[32,512]{1,0:T(8,128)S(1)}, f32[32,512]{1,0:T(8,128)S(1)}, u32[]{:S(2)}, u32[]{:S(2)}) collective-permute-start(f32[32,512]{1,0:T(8,128)S(1)} %get-tuple-element.17), channel_id=1, source_target_pairs={{0,8},{1,9},{2,10},{3,11},{4,12},{5,13},{6,14},{7,15},{8,0},{9,1},... | collective-permute-start | bytes 196616 | tf_op jit(solution)/shard_map/ppermute | solution.py:149
  4.5 5.3 %collective-permute-start.1 = (f32[32,512]{1,0:T(8,128)S(1)}, f32[32,512]{1,0:T(8,128)S(1)}, u32[]{:S(2)}, u32[]{:S(2)}) collective-permute-start(f32[32,512]{1,0:T(8,128)S(1)} %add.30), channel_id=1, source_target_pairs={{0,1},{1,0},{2,3},{3,2},{4,5},{5,4},{6,7},{7,6},{8,9},{9,8},{10,11... | collective-permute-start | bytes 196616 | tf_op jit(solution)/shard_map/ppermute | solution.py:149
  7.4 4.4 %collective-permute-start.7 = (f32[32,512]{1,0:T(8,128)S(1)}, f32[32,512]{1,0:T(8,128)S(1)}, u32[]{:S(2)}, u32[]{:S(2)}) collective-permute-start(f32[32,512]{1,0:T(8,128)S(1)} %add.35), channel_id=1, source_target_pairs={{0,2},{1,3},{2,0},{3,1},{4,6},{5,7},{6,4},{7,5},{8,10},{9,11},{10,... | collective-permute-start | bytes 196616 | tf_op jit(solution)/shard_map/ppermute | solution.py:149
  9.8 4.6 %collective-permute-start.2 = (f32[32,512]{1,0:T(8,128)S(1)}, f32[32,512]{1,0:T(8,128)S(1)}, u32[]{:S(2)}, u32[]{:S(2)}) collective-permute-start(f32[32,512]{1,0:T(8,128)S(1)} %add.31), channel_id=1, source_target_pairs={{0,16},{1,17},{2,18},{3,19},{4,20},{5,21},{6,22},{7,23},{8,24},{9,... | collective-permute-start | bytes 196616 | tf_op jit(solution)/shard_map/ppermute | solution.py:149
  11.7 5.2 %collective-permute-start.8 = (f32[32,512]{1,0:T(8,128)S(1)}, f32[32,512]{1,0:T(8,128)S(1)}, u32[]{:S(2)}, u32[]{:S(2)}) collective-permute-start(f32[32,512]{1,0:T(8,128)S(1)} %add.36), channel_id=1, source_target_pairs={{0,4},{1,5},{2,6},{3,7},{4,0},{5,1},{6,2},{7,3},{8,12},{9,13},{10,... | collective-permute-start | bytes 196616 | tf_op jit(solution)/shard_map/ppermute | solution.py:149
  14.4 4.3 %collective-permute-start.3 = (f32[32,512]{1,0:T(8,128)S(1)}, f32[32,512]{1,0:T(8,128)S(1)}, u32[]{:S(2)}, u32[]{:S(2)}) collective-permute-start(f32[32,512]{1,0:T(8,128)S(1)} %add.32), channel_id=1, source_target_pairs={{0,2},{1,3},{2,0},{3,1},{4,6},{5,7},{6,4},{7,5},{8,10},{9,11},{10,... | collective-permute-start | bytes 196616 | tf_op jit(solution)/shard_map/ppermute | solution.py:149
  17.0 4.5 %collective-permute-start.9 = (f32[32,512]{1,0:T(8,128)S(1)}, f32[32,512]{1,0:T(8,128)S(1)}, u32[]{:S(2)}, u32[]{:S(2)}) collective-permute-start(f32[32,512]{1,0:T(8,128)S(1)} %add.37), channel_id=1, source_target_pairs={{0,1},{1,0},{2,3},{3,2},{4,5},{5,4},{6,7},{7,6},{8,9},{9,8},{10,11... | collective-permute-start | bytes 196616 | tf_op jit(solution)/shard_map/ppermute | solution.py:149
  18.8 5.2 %collective-permute-start.4 = (f32[32,512]{1,0:T(8,128)S(1)}, f32[32,512]{1,0:T(8,128)S(1)}, u32[]{:S(2)}, u32[]{:S(2)}) collective-permute-start(f32[32,512]{1,0:T(8,128)S(1)} %add.33), channel_id=1, source_target_pairs={{0,4},{1,5},{2,6},{3,7},{4,0},{5,1},{6,2},{7,3},{8,12},{9,13},{10,... | collective-permute-start | bytes 196616 | tf_op jit(solution)/shard_map/ppermute | solution.py:149
  21.5 4.3 %collective-permute-start.10 = (f32[32,512]{1,0:T(8,128)S(1)}, f32[32,512]{1,0:T(8,128)S(1)}, u32[]{:S(2)}, u32[]{:S(2)}) collective-permute-start(f32[32,512]{1,0:T(8,128)S(1)} %add.38), channel_id=1, source_target_pairs={{0,16},{1,17},{2,18},{3,19},{4,20},{5,21},{6,22},{7,23},{8,24},{9,... | collective-permute-start | bytes 196616 | tf_op jit(solution)/shard_map/ppermute | solution.py:149
  24.0 1.9 %collective-permute-start.5 = (f32[32,512]{1,0:T(8,128)S(1)}, f32[32,512]{1,0:T(8,128)S(1)}, u32[]{:S(2)}, u32[]{:S(2)}) collective-permute-start(f32[32,512]{1,0:T(8,128)S(1)} %add.34.refs_0_), channel_id=1, source_target_pairs={{0,8},{1,9},{2,10},{3,11},{4,12},{5,13},{6,14},{7,15},{8,0},{9,1},... | collective-permute-start | bytes 196616 | tf_op jit(solution)/shard_map/ppermute | solution.py:149
  25.9 1.3 %collective-permute-start.11 = (f32[32,512]{1,0:T(8,128)S(1)}, f32[32,512]{1,0:T(8,128)S(1)}, u32[]{:S(2)}, u32[]{:S(2)}) collective-permute-start(f32[32,512]{1,0:T(8,128)S(1)} %add.39.refs_2_), channel_id=1, source_target_pairs={{0,8},{1,9},{2,10},{3,11},{4,12},{5,13},{6,14},{7,15},{8,0},{9,1},... | collective-permute-start | bytes 196616 | tf_op jit(solution)/shard_map/ppermute | solution.py:149

commit v4 on v3

--- a/solution.py
+++ b/solution.py
@@ -8,7 +8,6 @@
 from jax.sharding import PartitionSpec as P
 
 AXES = ("group", "dev")
-WINDOW = 5
 
 
 def pick_kernel(pivots_ref, points_hbm, base_hbm, *refs):
@@ -48,6 +47,7 @@
 def dot(a, b, dims):
     return lax.dot_general(a, b, ((dims[:1], dims[1:]), ((), ())), preferred_element_type=jnp.float32)
 
+
 def split(value):
     high = value.astype(jnp.bfloat16)
     rest = value - high.astype(jnp.float32)
@@ -55,6 +55,7 @@
     low = (rest - middle.astype(jnp.float32)).astype(jnp.bfloat16)
     return high, middle, low
 
+
 def product_nt(a, b):
     n = a[0].shape[0]
     first = dot(jnp.concatenate(a, axis=0), b[0], (1, 1))
@@ -62,14 +63,19 @@
     third = dot(a[0], b[2], (1, 1))
     return first[:n] + (first[n:2*n] + second[:n]) + (first[2*n:] + second[n:] + third)
 
-def gram_tn(upper, split_at):
-    h, m, l = split(upper)
-    left = jnp.concatenate([x[:, :split_at] for x in (h, m, h, l, m, h)], axis=0)
-    right = jnp.concatenate([h, h, m, h, m, l], axis=0)
-    return dot(left, right, (0, 0))
+
+def terms(value, axis, left):
+    h, m, l = split(value)
+    return jnp.concatenate((h, m, h, l, m, h) if left else (h, h, m, h, m, l), axis=axis)
+
+
+def ahead(column):
+    return 4 + column // 12
+
 
 def spread(tile, sub):
     return jnp.broadcast_to(tile[sub:sub + 1, :], (8, 128))
+
 
 def eliminate(panel, lane0):
     groups, tiles = len(panel), len(panel[0])
@@ -78,11 +84,15 @@
 
     def column(c):
         lane = lane0 + c
-        return [jnp.broadcast_to(panel[g][0][:, lane:lane + 1], (8, 128)) if g >= c // 8 else None for g in range(groups)]
-
-    rep = {c: column(c) for c in range(min(WINDOW + 1, b))}
+        return [jnp.broadcast_to(panel[g][0][:, lane : lane + 1], (8, 128)) if g >= c // 8 else None for g in range(groups)]
+
+    rep = {}
+    fresh = 0
     roots = [jnp.zeros((8, 128), jnp.float32) for _ in range(groups)]
     for j in range(b):
+        while fresh < b and fresh - ahead(fresh) <= j:
+            rep[fresh] = column(fresh)
+            fresh += 1
         gj, sj = j // 8, j % 8
         mine = rep.pop(j)
         pivot = spread(mine[gj], sj)
@@ -90,7 +100,7 @@
         roots[gj] = jnp.where(row_id == sj, lax.rsqrt(pivot), roots[gj])
         weight = [None if g < gj else mine[g] * inverse for g in range(groups)]
         weight[gj] = jnp.where(row_id > sj, weight[gj], 0.0)
-        for c in range(j + 1, min(j + WINDOW + 1, b)):
+        for c in sorted(rep):
             entry = spread(mine[c // 8], c % 8)
             for g in range(c // 8, groups):
                 rep[c][g] = rep[c][g] - weight[g] * entry
@@ -98,46 +108,78 @@
             line = spread(panel[gj][t], sj)
             for g in range(gj, groups):
                 panel[g][t] = panel[g][t] - weight[g] * line
-        if j + WINDOW + 1 < b:
-            rep[j + WINDOW + 1] = column(j + WINDOW + 1)
     return [[panel[g][t] * roots[g] for t in range(tiles)] for g in range(groups)]
+
 
 def join(tiles):
     return jnp.concatenate([jnp.concatenate(row, axis=1) for row in tiles], axis=0)
 
+
 def tiles_of(ref, row, count, tile0, tiles):
     return [[ref[row + 8 * g:row + 8 * g + 8, 128 * t:128 * t + 128] for t in range(tile0, tiles)] for g in range(count // 8)]
 
-def factor_kernel(*refs):
-    parts, local, (cols_ref, diag_ref, pivot_ref, work_ref) = refs[:-10], refs[-10:-4], refs[-4:]
-    points_ref, high_ref, middle_ref, low_ref, norms_ref, start_ref = local
-    part = parts[0].shape[0]
-    total = part * len(parts)
-    rows, dim = points_ref.shape
+
+def kernel_rows(inner, row_norms, lane_norms, dim):
+    return jnp.exp((-2.0 / dim) * (row_norms + lane_norms - 2.0 * inner))
+
+
+def gather_rows(target, mine, other):
+    part = mine.shape[0]
     core = lax.axis_index("group") % 2
-    for i in range(0, len(parts), 2):
-        pivot_ref[pl.ds(pl.multiple_of((i + core) * part, part), part), :] = parts[i][...]
-        pivot_ref[pl.ds(pl.multiple_of((i + 1 - core) * part, part), part), :] = parts[i + 1][...]
-    points = points_ref[...]
-    base_parts = high_ref[...], middle_ref[...], low_ref[...]
-    norms = norms_ref[...]
-    centres = pivot_ref[:, :dim].astype(jnp.bfloat16)
-    pivot_base = split(pivot_ref[:, dim:])
+    target[pl.ds(pl.multiple_of(core * part, part), part), :] = mine[...]
+    target[pl.ds(pl.multiple_of((1 - core) * part, part), part), :] = other[...]
+
+
+def first_kernel(mine, other, points_ref, high_ref, middle_ref, low_ref, norms_ref, centres_ref, pieces_ref, norm_ref, inverse_ref, cols_ref, rows_ref, work_ref):
+    gather_rows(rows_ref, mine, other)
+    dim = points_ref.shape[1]
+    size = rows_ref.shape[0]
+    centres = rows_ref[:, :dim].astype(jnp.bfloat16)
+    pieces = split(rows_ref[:, dim:])
+    centres_ref[...] = centres
+    pieces_ref[...] = jnp.concatenate(pieces, axis=0)
     gram = dot(centres, centres, (1, 1))
-    eye = lax.broadcasted_iota(jnp.int32, (total, total), 0) == lax.broadcasted_iota(jnp.int32, (total, total), 1)
+    eye = lax.broadcasted_iota(jnp.int32, (size, size), 0) == lax.broadcasted_iota(jnp.int32, (size, size), 1)
+    own = jnp.where(eye, gram, 0.0)
+    norm_lane = jnp.sum(own, axis=0, keepdims=True)
+    norm_row = jnp.broadcast_to(jnp.sum(own, axis=1, keepdims=True), (size, 128))
+    norm_ref[...] = norm_row
+    work_ref[:, :size] = kernel_rows(gram, norm_row[:, :1], norm_lane, dim) - product_nt(pieces, pieces)
+    work_ref[:, size : 2 * size] = eye.astype(jnp.float32)
+    inner = dot(centres, points_ref[...], (1, 1))
+    base = high_ref[...], middle_ref[...], low_ref[...]
+    work_ref[:, 128:] = kernel_rows(inner, norm_row[:, :1], norms_ref[...], dim) - product_nt(pieces, base)
+    upper = join(eliminate(tiles_of(work_ref, 0, size, 0, work_ref.shape[1] // 128), 0))
+    inverse_ref[...] = terms(upper[:, size : 2 * size], 1, True)
+    cols_ref[...] = upper[:, 128:]
+
+
+def second_kernel(mine, other, points_ref, high_ref, middle_ref, low_ref, norms_ref, start_ref, centres_ref, pieces_ref, norm_ref, inverse_ref, before_ref, cols_ref, diag_ref, rows_ref, work_ref):
+    gather_rows(rows_ref, mine, other)
+    dim = points_ref.shape[1]
+    size = rows_ref.shape[0]
+    centres = rows_ref[:, :dim].astype(jnp.bfloat16)
+    pieces = split(rows_ref[:, dim:])
+    before = before_ref[...]
+    old = tuple(pieces_ref[k * size : (k + 1) * size, :] for k in range(3))
+    cross = dot(centres_ref[...], centres, (1, 1))
+    gram = dot(centres, centres, (1, 1))
+    eye = lax.broadcasted_iota(jnp.int32, (size, size), 0) == lax.broadcasted_iota(jnp.int32, (size, size), 1)
     own = jnp.where(eye, gram, 0.0)
     norm_lane = jnp.sum(own, axis=0, keepdims=True)
     norm_row = jnp.sum(own, axis=1, keepdims=True)
-    scale = -2.0 / dim
-    work_ref[:, :total] = jnp.exp(scale * (norm_row + norm_lane - 2.0 * gram)) - product_nt(pivot_base, pivot_base)
-    inner = dot(centres, points, (1, 1))
-    work_ref[:, total:] = jnp.exp(scale * (norm_row + norms - 2.0 * inner)) - product_nt(pivot_base, base_parts)
-    half = total // 2
-    count = (total + rows) // 128
-    top = join(eliminate(tiles_of(work_ref, 0, half, 0, count), 0))
-    work_ref[half:, :] = work_ref[half:, :] - gram_tn(top, total)[half:, :]
-    bottom = join(eliminate(tiles_of(work_ref, half, half, 0, count), half))
-    cols = jnp.concatenate([top[:, total:], bottom[:, total:]], axis=0)
+    cross = kernel_rows(cross, norm_ref[...][:, :1], norm_lane, dim) - product_nt(old, pieces)
+    share = dot(inverse_ref[...], terms(cross, 0, False), (1, 0))
+    block = kernel_rows(gram, norm_row, norm_lane, dim) - product_nt(pieces, pieces)
+    inner = dot(centres, points_ref[...], (1, 1))
+    base = high_ref[...], middle_ref[...], low_ref[...]
+    resid = kernel_rows(inner, norm_row, norms_ref[...], dim) - product_nt(pieces, base)
+    left = terms(share, 0, True)
+    work_ref[:, :size] = block - dot(left, terms(share, 0, False), (0, 0))
+    work_ref[:, size : 2 * size] = eye.astype(jnp.float32)
+    work_ref[:, 128:] = resid - dot(left, terms(before, 0, False), (0, 0))
+    upper = join(eliminate(tiles_of(work_ref, 0, size, 0, work_ref.shape[1] // 128), 0))
+    cols = jnp.concatenate([before, upper[:, 128:]], axis=0)
     cols_ref[...] = cols.T
     diag_ref[...] = start_ref[...] - jnp.sum(cols * cols, axis=0, keepdims=True)
 
@@ -191,22 +233,37 @@
     )(pivots, points, base_factor)
     chains, local = chains[:n], chains[n:]
     parts = exchange(chains, mesh)
-    total = rounds * slots
+    width = dim + base
+    half = jnp.bfloat16
+    scratch = [pltpu.VMEM((slots, width), jnp.float32), pltpu.VMEM((slots, 128 + rows), jnp.float32)]
+    front = pl.pallas_call(
+        first_kernel,
+        out_shape=(
+            jax.ShapeDtypeStruct((slots, dim), half),
+            jax.ShapeDtypeStruct((3 * slots, base), half),
+            jax.ShapeDtypeStruct((slots, 128), jnp.float32),
+            jax.ShapeDtypeStruct((slots, 6 * slots), half),
+            jax.ShapeDtypeStruct((slots, rows), jnp.float32),
+        ),
+        in_specs=vmem(7),
+        out_specs=tuple(vmem(5)),
+        scratch_shapes=scratch,
+        compiler_params=pltpu.CompilerParams(vmem_limit_bytes=16 * 2**20),
+        cost_estimate=pl.CostEstimate(flops=10**7, bytes_accessed=2**19, transcendentals=0),
+        name="first",
+    )(*parts[:2], *local[:5])
     cols, diag = pl.pallas_call(
-        factor_kernel,
+        second_kernel,
         out_shape=(
-            jax.ShapeDtypeStruct((rows, total), jnp.float32),
+            jax.ShapeDtypeStruct((rows, 2 * slots), jnp.float32),
             jax.ShapeDtypeStruct((1, rows), jnp.float32),
         ),
-        in_specs=vmem(n + 6),
+        in_specs=vmem(13),
         out_specs=tuple(vmem(2)),
-        scratch_shapes=[
-            pltpu.VMEM((total, dim + base), jnp.float32),
-            pltpu.VMEM((total, total + rows), jnp.float32),
-        ],
+        scratch_shapes=scratch,
         compiler_params=pltpu.CompilerParams(vmem_limit_bytes=16 * 2**20),
-        name="factor",
-    )(*parts, *local)
+        name="second",
+    )(*parts[2:], *local, *front)
     return cols, diag.reshape(rows)
 
 

time: 31.1 us -> 30.3 us (0.974)
  waiting for transfers between devices: 6.28 us -> 5.05 us
  Pallas kernels: 5.48 us -> 5.85 us
    ppermute x12, waiting for transfers between devices: 6.28 us -> 5.05 us  [swap(): lax.ppermute(value, AXES, [(i, partner(i)) for i in range(groups * devs)])]
    pallas_call x1 -> x2, Pallas kernels: 3.81 us -> 4.18 us  [the longest x1 2.59 us: per_device(): pl.pallas_call(second_kernel, out_shape=(jax.ShapeDtypeStruct((rows, 2 *...]
  transfers between devices with their start and end apart: 12 -> 12, of which waited for: 7 -> 6; matrix products, arithmetic and copies ran while one was open for 0% -> 0% of each run, Pallas kernels for 0% -> 5%
where the time goes in v4:
time: 30.3 us; the launch traced here: 30.1 us
  starting transfers between devices  17.7 us (58%)
  Pallas kernels  5.85 us (19%)
  waiting for transfers between devices  5.05 us (17%)
  between operations  0.71 us (2%)
  local copies, waits for them, and re-layouts  0.67 us (2%)
    ppermute x12, starting transfers between devices, swap(): lax.ppermute(value, AXES, [(i, partner(i)) for i in range(groups * devs)])  17.7 us
    ppermute x12, waiting for transfers between devices, swap(): lax.ppermute(value, AXES, [(i, partner(i)) for i in range(groups * devs)])  5.05 us
    pallas_call x1, Pallas kernels, per_device(): pl.pallas_call(second_kernel, out_shape=(jax.ShapeDtypeStruct((rows, 2 *...  2.59 us
    pallas_call x1, Pallas kernels, per_device(): pl.pallas_call(pick_kernel, out_shape=(piece,) * n + (jax.ShapeDtypeStruc...  1.67 us
    pallas_call x1, Pallas kernels, per_device(): pl.pallas_call(first_kernel, out_shape=(jax.ShapeDtypeStruct((slots, dim)...  1.59 us
    unnamed x2, local copies, waits for them, and re-layouts  0.67 us
  transfers between devices with their start and end apart: 12, of which 6 were waited for; matrix products, arithmetic and copies ran while one was open for 0% of the time, Pallas kernels for 5%

profile of v4, /device:TPU:0, one launch (start us, length us, event | category | flops | bytes accessed | tf_op | source)
XLA Modules:
  0.0 30.1 jit_solution(7680925035198360964)
XLA Ops:
  0.6 0.0 copy-start
  0.6 0.7 %copy-done = s32[2,64]{1,0:T(2,128)S(1)} copy-done((s32[2,64]{1,0:T(2,128)S(1)}, s32[2,64]{1,0:T(2,128)}, u32[]{:S(2)}) %copy-start) | copy-done | bytes 536
  1.3 1.7 %pick.1 = (f32[32,512]{1,0:T(8,128)S(1)}, f32[32,512]{1,0:T(8,128)S(1)}, f32[32,512]{1,0:T(8,128)S(1)}, f32[32,512]{1,0:T(8,128)S(1)}, bf16[256,256]{1,0:T(8,128...) custom-call(s32[2,64]{1,0:T(2,128)S(1)} %copy-done, ...), custom_call_target="tpu_custom_call" | custom-call | tf_op jit(solution)/shard_map/pick/pallas_call | solution.py:222
  3.0 0.6 %collective-permute-start.6 = (f32[32,512]{1,0:T(8,128)S(1)}, f32[32,512]{1,0:T(8,128)S(1)}, u32[]{:S(2)}, u32[]{:S(2)}) collective-permute-start(f32[32,512]{1,0:T(8,128)S(1)} %get-tuple-element.28), channel_id=1, source_target_pairs={{0,8},{1,9},{2,10},{3,11},{4,12},{5,13},{6,14},{7,15},{8,0},{9,1},... | collective-permute-start | bytes 196616 | tf_op jit(solution)/shard_map/ppermute | solution.py:191
  3.5 0.1 collective-permute-start
  3.6 0.8 %collective-permute-done.6 = f32[32,512]{1,0:T(8,128)S(1)} collective-permute-done((f32[32,512]{1,0:T(8,128)S(1)}, f32[32,512]{1,0:T(8,128)S(1)}, u32[]{:S(2)}, u32[]{:S(2)}) %collective-permute-start.6) | collective-permute-done | bytes 65568 | tf_op jit(solution)/shard_map/ppermute | solution.py:191
  4.5 2.9 %collective-permute-start.7 = (f32[32,512]{1,0:T(8,128)S(1)}, f32[32,512]{1,0:T(8,128)S(1)}, u32[]{:S(2)}, u32[]{:S(2)}) collective-permute-start(f32[32,512]{1,0:T(8,128)S(1)} %add.35), channel_id=1, source_target_pairs={{0,1},{1,0},{2,3},{3,2},{4,5},{5,4},{6,7},{7,6},{8,9},{9,8},{10,11... | collective-permute-start | bytes 196616 | tf_op jit(solution)/shard_map/ppermute | solution.py:191
  7.4 0.0 collective-permute-done
  7.4 1.6 %collective-permute-start.1 = (f32[32,512]{1,0:T(8,128)S(1)}, f32[32,512]{1,0:T(8,128)S(1)}, u32[]{:S(2)}, u32[]{:S(2)}) collective-permute-start(f32[32,512]{1,0:T(8,128)S(1)} %add.30), channel_id=1, source_target_pairs={{0,2},{1,3},{2,0},{3,1},{4,6},{5,7},{6,4},{7,5},{8,10},{9,11},{10,... | collective-permute-start | bytes 196616 | tf_op jit(solution)/shard_map/ppermute | solution.py:191
  9.0 0.8 %collective-permute-done.7 = f32[32,512]{1,0:T(8,128)S(1)} collective-permute-done((f32[32,512]{1,0:T(8,128)S(1)}, f32[32,512]{1,0:T(8,128)S(1)}, u32[]{:S(2)}, u32[]{:S(2)}) %collective-permute-start.7) | collective-permute-done | bytes 65568 | tf_op jit(solution)/shard_map/ppermute | solution.py:191
  9.8 1.9 %collective-permute-start.8 = (f32[32,512]{1,0:T(8,128)S(1)}, f32[32,512]{1,0:T(8,128)S(1)}, u32[]{:S(2)}, u32[]{:S(2)}) collective-permute-start(f32[32,512]{1,0:T(8,128)S(1)} %add.36), channel_id=1, source_target_pairs={{0,16},{1,17},{2,18},{3,19},{4,20},{5,21},{6,22},{7,23},{8,24},{9,... | collective-permute-start | bytes 196616 | tf_op jit(solution)/shard_map/ppermute | solution.py:191
  11.7 0.0 collective-permute-done.1
  11.7 2.7 %collective-permute-start.2 = (f32[32,512]{1,0:T(8,128)S(1)}, f32[32,512]{1,0:T(8,128)S(1)}, u32[]{:S(2)}, u32[]{:S(2)}) collective-permute-start(f32[32,512]{1,0:T(8,128)S(1)} %add.31), channel_id=1, source_target_pairs={{0,4},{1,5},{2,6},{3,7},{4,0},{5,1},{6,2},{7,3},{8,12},{9,13},{10,... | collective-permute-start | bytes 196616 | tf_op jit(solution)/shard_map/ppermute | solution.py:191
  14.4 0.0 collective-permute-done.8
  14.4 1.7 %collective-permute-start.9 = (f32[32,512]{1,0:T(8,128)S(1)}, f32[32,512]{1,0:T(8,128)S(1)}, u32[]{:S(2)}, u32[]{:S(2)}) collective-permute-start(f32[32,512]{1,0:T(8,128)S(1)} %add.37), channel_id=1, source_target_pairs={{0,2},{1,3},{2,0},{3,1},{4,6},{5,7},{6,4},{7,5},{8,10},{9,11},{10,... | collective-permute-start | bytes 196616 | tf_op jit(solution)/shard_map/ppermute | solution.py:191
  16.1 0.8 %collective-permute-done.2 = f32[32,512]{1,0:T(8,128)S(1)} collective-permute-done((f32[32,512]{1,0:T(8,128)S(1)}, f32[32,512]{1,0:T(8,128)S(1)}, u32[]{:S(2)}, u32[]{:S(2)}) %collective-permute-start.2) | collective-permute-done | bytes 65568 | tf_op jit(solution)/shard_map/ppermute | solution.py:191
  17.0 1.6 %collective-permute-start.3 = (f32[32,512]{1,0:T(8,128)S(1)}, f32[32,512]{1,0:T(8,128)S(1)}, u32[]{:S(2)}, u32[]{:S(2)}) collective-permute-start(f32[32,512]{1,0:T(8,128)S(1)} %add.32), channel_id=1, source_target_pairs={{0,1},{1,0},{2,3},{3,2},{4,5},{5,4},{6,7},{7,6},{8,9},{9,8},{10,11... | collective-permute-start | bytes 196616 | tf_op jit(solution)/shard_map/ppermute | solution.py:191
  18.5 0.2 collective-permute-done.9
  18.8 2.7 %collective-permute-start.10 = (f32[32,512]{1,0:T(8,128)S(1)}, f32[32,512]{1,0:T(8,128)S(1)}, u32[]{:S(2)}, u32[]{:S(2)}) collective-permute-start(f32[32,512]{1,0:T(8,128)S(1)} %add.38), channel_id=1, source_target_pairs={{0,4},{1,5},{2,6},{3,7},{4,0},{5,1},{6,2},{7,3},{8,12},{9,13},{10,... | collective-permute-start | bytes 196616 | tf_op jit(solution)/shard_map/ppermute | solution.py:191
  21.5 0.0 collective-permute-done.3
  21.5 1.8 %collective-permute-start.4 = (f32[32,512]{1,0:T(8,128)S(1)}, f32[32,512]{1,0:T(8,128)S(1)}, u32[]{:S(2)}, u32[]{:S(2)}) collective-permute-start(f32[32,512]{1,0:T(8,128)S(1)} %add.33), channel_id=1, source_target_pairs={{0,16},{1,17},{2,18},{3,19},{4,20},{5,21},{6,22},{7,23},{8,24},{9,... | collective-permute-start | bytes 196616 | tf_op jit(solution)/shard_map/ppermute | solution.py:191
  23.3 0.7 %collective-permute-done.10 = f32[32,512]{1,0:T(8,128)S(1)} collective-permute-done((f32[32,512]{1,0:T(8,128)S(1)}, f32[32,512]{1,0:T(8,128)S(1)}, u32[]{:S(2)}, u32[]{:S(2)}) %collective-permute-start.10) | collective-permute-done | bytes 65568 | tf_op jit(solution)/shard_map/ppermute | solution.py:191
  24.0 0.1 collective-permute-start.11
  24.1 1.8 %collective-permute-done.4 = f32[32,512]{1,0:T(8,128)S(1)} collective-permute-done((f32[32,512]{1,0:T(8,128)S(1)}, f32[32,512]{1,0:T(8,128)S(1)}, u32[]{:S(2)}, u32[]{:S(2)}) %collective-permute-start.4) | collective-permute-done | bytes 65568 | tf_op jit(solution)/shard_map/ppermute | solution.py:191
  25.9 0.1 collective-permute-start.5
  25.9 0.0 collective-permute-done.11.other
  25.9 1.6 %first.1 = (bf16[64,256]{1,0:T(8,128)(2,1)S(1)}, bf16[192,256]{1,0:T(8,128)(2,1)S(1)}, f32[64,128]{1,0:T(8,128)S(1)}, bf16[64,384]{1,0:T(8,128)(2,1)S(1)}, f32[64,256]{1,0:T(8,128)S(1)}) custom-call(f32[32,512]{1,0:T(8,128)S(1)} %add.39.mine, f32[32,512]{1,0:T(8,128)S(1)} %collective-permute-done.11.other, ...), custom_call_target="tpu_custom_call" | custom-call | flops 10000000 | bytes 524288 | tf_op jit(solution)/shard_map/first/pallas_call | solution.py:239
  27.5 0.0 collective-permute-done.5.other
  27.5 2.6 %second.1 = (f32[256,128]{1,0:T(8,128)}, f32[1,256]{1,0:T(1,128)}) custom-call(f32[32,512]{1,0:T(8,128)S(1)} %add.34.mine, f32[32,512]{1,0:T(8,128)S(1)} %collective-permute-done.5.other, bf16[256,256]{1,0:T(8,128)(2,1)S(1)} %get-tuple-element.21.points_ref, bf16[256,256]{1,0:T(8,128)(2,1)S(1)} %get-tuple-element.22.high_ref, ...), custom_call_target="tpu_custom_call" | custom-call | tf_op jit(solution)/shard_map/second/pallas_call | solution.py:255
  (10 shorter events, 0.1 us)
Async XLA Ops:
  0.6 0.7 %copy-start = (s32[2,64]{1,0:T(2,128)S(1)}, s32[2,64]{1,0:T(2,128)}, u32[]{:S(2)}) copy-start(s32[2,64]{1,0:T(2,128)} %pivots_ref.1) | copy-start | bytes 1540
  3.0 1.5 %collective-permute-start.6 = (f32[32,512]{1,0:T(8,128)S(1)}, f32[32,512]{1,0:T(8,128)S(1)}, u32[]{:S(2)}, u32[]{:S(2)}) collective-permute-start(f32[32,512]{1,0:T(8,128)S(1)} %get-tuple-element.28), channel_id=1, source_target_pairs={{0,8},{1,9},{2,10},{3,11},{4,12},{5,13},{6,14},{7,15},{8,0},{9,1},... | collective-permute-start | bytes 196616 | tf_op jit(solution)/shard_map/ppermute | solution.py:191
  3.5 3.8 %collective-permute-start = (f32[32,512]{1,0:T(8,128)S(1)}, f32[32,512]{1,0:T(8,128)S(1)}, u32[]{:S(2)}, u32[]{:S(2)}) collective-permute-start(f32[32,512]{1,0:T(8,128)S(1)} %get-tuple-element.20), channel_id=1, source_target_pairs={{0,8},{1,9},{2,10},{3,11},{4,12},{5,13},{6,14},{7,15},{8,0},{9,1},... | collective-permute-start | bytes 196616 | tf_op jit(solution)/shard_map/ppermute | solution.py:191
  4.5 5.3 %collective-permute-start.7 = (f32[32,512]{1,0:T(8,128)S(1)}, f32[32,512]{1,0:T(8,128)S(1)}, u32[]{:S(2)}, u32[]{:S(2)}) collective-permute-start(f32[32,512]{1,0:T(8,128)S(1)} %add.35), channel_id=1, source_target_pairs={{0,1},{1,0},{2,3},{3,2},{4,5},{5,4},{6,7},{7,6},{8,9},{9,8},{10,11... | collective-permute-start | bytes 196616 | tf_op jit(solution)/shard_map/ppermute | solution.py:191
  7.4 4.4 %collective-permute-start.1 = (f32[32,512]{1,0:T(8,128)S(1)}, f32[32,512]{1,0:T(8,128)S(1)}, u32[]{:S(2)}, u32[]{:S(2)}) collective-permute-start(f32[32,512]{1,0:T(8,128)S(1)} %add.30), channel_id=1, source_target_pairs={{0,2},{1,3},{2,0},{3,1},{4,6},{5,7},{6,4},{7,5},{8,10},{9,11},{10,... | collective-permute-start | bytes 196616 | tf_op jit(solution)/shard_map/ppermute | solution.py:191
  9.8 4.6 %collective-permute-start.8 = (f32[32,512]{1,0:T(8,128)S(1)}, f32[32,512]{1,0:T(8,128)S(1)}, u32[]{:S(2)}, u32[]{:S(2)}) collective-permute-start(f32[32,512]{1,0:T(8,128)S(1)} %add.36), channel_id=1, source_target_pairs={{0,16},{1,17},{2,18},{3,19},{4,20},{5,21},{6,22},{7,23},{8,24},{9,... | collective-permute-start | bytes 196616 | tf_op jit(solution)/shard_map/ppermute | solution.py:191
  11.7 5.2 %collective-permute-start.2 = (f32[32,512]{1,0:T(8,128)S(1)}, f32[32,512]{1,0:T(8,128)S(1)}, u32[]{:S(2)}, u32[]{:S(2)}) collective-permute-start(f32[32,512]{1,0:T(8,128)S(1)} %add.31), channel_id=1, source_target_pairs={{0,4},{1,5},{2,6},{3,7},{4,0},{5,1},{6,2},{7,3},{8,12},{9,13},{10,... | collective-permute-start | bytes 196616 | tf_op jit(solution)/shard_map/ppermute | solution.py:191
  14.4 4.3 %collective-permute-start.9 = (f32[32,512]{1,0:T(8,128)S(1)}, f32[32,512]{1,0:T(8,128)S(1)}, u32[]{:S(2)}, u32[]{:S(2)}) collective-permute-start(f32[32,512]{1,0:T(8,128)S(1)} %add.37), channel_id=1, source_target_pairs={{0,2},{1,3},{2,0},{3,1},{4,6},{5,7},{6,4},{7,5},{8,10},{9,11},{10,... | collective-permute-start | bytes 196616 | tf_op jit(solution)/shard_map/ppermute | solution.py:191
  17.0 4.5 %collective-permute-start.3 = (f32[32,512]{1,0:T(8,128)S(1)}, f32[32,512]{1,0:T(8,128)S(1)}, u32[]{:S(2)}, u32[]{:S(2)}) collective-permute-start(f32[32,512]{1,0:T(8,128)S(1)} %add.32), channel_id=1, source_target_pairs={{0,1},{1,0},{2,3},{3,2},{4,5},{5,4},{6,7},{7,6},{8,9},{9,8},{10,11... | collective-permute-start | bytes 196616 | tf_op jit(solution)/shard_map/ppermute | solution.py:191
  18.8 5.2 %collective-permute-start.10 = (f32[32,512]{1,0:T(8,128)S(1)}, f32[32,512]{1,0:T(8,128)S(1)}, u32[]{:S(2)}, u32[]{:S(2)}) collective-permute-start(f32[32,512]{1,0:T(8,128)S(1)} %add.38), channel_id=1, source_target_pairs={{0,4},{1,5},{2,6},{3,7},{4,0},{5,1},{6,2},{7,3},{8,12},{9,13},{10,... | collective-permute-start | bytes 196616 | tf_op jit(solution)/shard_map/ppermute | solution.py:191
  21.5 4.3 %collective-permute-start.4 = (f32[32,512]{1,0:T(8,128)S(1)}, f32[32,512]{1,0:T(8,128)S(1)}, u32[]{:S(2)}, u32[]{:S(2)}) collective-permute-start(f32[32,512]{1,0:T(8,128)S(1)} %add.33), channel_id=1, source_target_pairs={{0,16},{1,17},{2,18},{3,19},{4,20},{5,21},{6,22},{7,23},{8,24},{9,... | collective-permute-start | bytes 196616 | tf_op jit(solution)/shard_map/ppermute | solution.py:191
  24.0 1.9 %collective-permute-start.11 = (f32[32,512]{1,0:T(8,128)S(1)}, f32[32,512]{1,0:T(8,128)S(1)}, u32[]{:S(2)}, u32[]{:S(2)}) collective-permute-start(f32[32,512]{1,0:T(8,128)S(1)} %add.39.mine), channel_id=1, source_target_pairs={{0,8},{1,9},{2,10},{3,11},{4,12},{5,13},{6,14},{7,15},{8,0},{9,1},... | collective-permute-start | bytes 196616 | tf_op jit(solution)/shard_map/ppermute | solution.py:191
  25.9 1.7 %collective-permute-start.5 = (f32[32,512]{1,0:T(8,128)S(1)}, f32[32,512]{1,0:T(8,128)S(1)}, u32[]{:S(2)}, u32[]{:S(2)}) collective-permute-start(f32[32,512]{1,0:T(8,128)S(1)} %add.34.mine), channel_id=1, source_target_pairs={{0,8},{1,9},{2,10},{3,11},{4,12},{5,13},{6,14},{7,15},{8,0},{9,1},... | collective-permute-start | bytes 196616 | tf_op jit(solution)/shard_map/ppermute | solution.py:191

commit v5 on v4

--- a/solution.py
+++ b/solution.py
@@ -6,6 +6,7 @@
 from jax.experimental import pallas as pl
 from jax.experimental.pallas import tpu as pltpu
 from jax.sharding import PartitionSpec as P
+
 
 AXES = ("group", "dev")
 
@@ -130,7 +131,7 @@
     target[pl.ds(pl.multiple_of((1 - core) * part, part), part), :] = other[...]
 
 
-def first_kernel(mine, other, points_ref, high_ref, middle_ref, low_ref, norms_ref, centres_ref, pieces_ref, norm_ref, inverse_ref, cols_ref, rows_ref, work_ref):
+def zero_kernel(mine, other, points_ref, high_ref, middle_ref, low_ref, norms_ref, centres_ref, pieces_ref, norm_ref, work_ref, rows_ref):
     gather_rows(rows_ref, mine, other)
     dim = points_ref.shape[1]
     size = rows_ref.shape[0]
@@ -149,6 +150,10 @@
     inner = dot(centres, points_ref[...], (1, 1))
     base = high_ref[...], middle_ref[...], low_ref[...]
     work_ref[:, 128:] = kernel_rows(inner, norm_row[:, :1], norms_ref[...], dim) - product_nt(pieces, base)
+
+
+def first_kernel(work_ref, inverse_ref, cols_ref):
+    size = work_ref.shape[0]
     upper = join(eliminate(tiles_of(work_ref, 0, size, 0, work_ref.shape[1] // 128), 0))
     inverse_ref[...] = terms(upper[:, size : 2 * size], 1, True)
     cols_ref[...] = upper[:, 128:]
@@ -236,22 +241,30 @@
     width = dim + base
     half = jnp.bfloat16
     scratch = [pltpu.VMEM((slots, width), jnp.float32), pltpu.VMEM((slots, 128 + rows), jnp.float32)]
-    front = pl.pallas_call(
-        first_kernel,
+    *front, work = pl.pallas_call(
+        zero_kernel,
         out_shape=(
             jax.ShapeDtypeStruct((slots, dim), half),
             jax.ShapeDtypeStruct((3 * slots, base), half),
             jax.ShapeDtypeStruct((slots, 128), jnp.float32),
-            jax.ShapeDtypeStruct((slots, 6 * slots), half),
-            jax.ShapeDtypeStruct((slots, rows), jnp.float32),
+            jax.ShapeDtypeStruct((slots, 128 + rows), jnp.float32),
         ),
         in_specs=vmem(7),
-        out_specs=tuple(vmem(5)),
-        scratch_shapes=scratch,
+        out_specs=tuple(vmem(4)),
+        scratch_shapes=scratch[:1],
+        compiler_params=pltpu.CompilerParams(vmem_limit_bytes=16 * 2**20),
+        cost_estimate=pl.CostEstimate(flops=10**7, bytes_accessed=2**19, transcendentals=0),
+        name="blocks",
+    )(*parts[:2], *local[:5])
+    front += pl.pallas_call(
+        first_kernel,
+        out_shape=(jax.ShapeDtypeStruct((slots, 6 * slots), half), jax.ShapeDtypeStruct((slots, rows), jnp.float32)),
+        in_specs=vmem(1),
+        out_specs=tuple(vmem(2)),
         compiler_params=pltpu.CompilerParams(vmem_limit_bytes=16 * 2**20),
         cost_estimate=pl.CostEstimate(flops=10**7, bytes_accessed=2**19, transcendentals=0),
         name="first",
-    )(*parts[:2], *local[:5])
+    )(work)
     cols, diag = pl.pallas_call(
         second_kernel,
         out_shape=(

time: 30.3 us -> 30.3 us (level)
    pallas_call x1 -> x2, Pallas kernels: 1.59 us -> 1.64 us  [the longest x1 1.26 us: per_device(): pl.pallas_call(first_kernel, out_shape=(jax.ShapeDtypeStruct((slots, 6 *...]
where the time goes in v5:
time: 30.3 us; the launch traced here: 30.2 us
  starting transfers between devices  17.7 us (58%)
  Pallas kernels  5.9 us (19%)
  waiting for transfers between devices  5.05 us (17%)
  between operations  0.72 us (2%)
  local copies, waits for them, and re-layouts  0.67 us (2%)
    ppermute x12, starting transfers between devices, swap(): lax.ppermute(value, AXES, [(i, partner(i)) for i in range(groups * devs)])  17.7 us
    ppermute x12, waiting for transfers between devices, swap(): lax.ppermute(value, AXES, [(i, partner(i)) for i in range(groups * devs)])  5.05 us
    pallas_call x1, Pallas kernels, per_device(): pl.pallas_call(second_kernel, out_shape=(jax.ShapeDtypeStruct((rows, 2 *...  2.59 us
    pallas_call x1, Pallas kernels, per_device(): pl.pallas_call(pick_kernel, out_shape=(piece,) * n + (jax.ShapeDtypeStruc...  1.67 us
    pallas_call x1, Pallas kernels, per_device(): pl.pallas_call(first_kernel, out_shape=(jax.ShapeDtypeStruct((slots, 6 *...  1.26 us
    unnamed x2, local copies, waits for them, and re-layouts  0.67 us
  transfers between devices with their start and end apart: 12, of which 6 were waited for; matrix products, arithmetic and copies ran while one was open for 0% of the time, Pallas kernels for 5%

profile of v5, /device:TPU:0, one launch (start us, length us, event | category | flops | bytes accessed | tf_op | source)
XLA Modules:
  0.0 30.2 jit_solution(9090852308340951792)
XLA Ops:
  0.6 0.0 copy-start
  0.6 0.7 %copy-done = s32[2,64]{1,0:T(2,128)S(1)} copy-done((s32[2,64]{1,0:T(2,128)S(1)}, s32[2,64]{1,0:T(2,128)}, u32[]{:S(2)}) %copy-start) | copy-done | bytes 536
  1.3 1.7 %pick.1 = (f32[32,512]{1,0:T(8,128)S(1)}, f32[32,512]{1,0:T(8,128)S(1)}, f32[32,512]{1,0:T(8,128)S(1)}, f32[32,512]{1,0:T(8,128)S(1)}, bf16[256,256]{1,0:T(8,128...) custom-call(s32[2,64]{1,0:T(2,128)S(1)} %copy-done, ...), custom_call_target="tpu_custom_call" | custom-call | tf_op jit(solution)/shard_map/pick/pallas_call | solution.py:227
  3.0 0.6 %collective-permute-start.6 = (f32[32,512]{1,0:T(8,128)S(1)}, f32[32,512]{1,0:T(8,128)S(1)}, u32[]{:S(2)}, u32[]{:S(2)}) collective-permute-start(f32[32,512]{1,0:T(8,128)S(1)} %get-tuple-element.29), channel_id=1, source_target_pairs={{0,8},{1,9},{2,10},{3,11},{4,12},{5,13},{6,14},{7,15},{8,0},{9,1},... | collective-permute-start | bytes 196616 | tf_op jit(solution)/shard_map/ppermute | solution.py:196
  3.5 0.1 collective-permute-start
  3.6 0.8 %collective-permute-done.6 = f32[32,512]{1,0:T(8,128)S(1)} collective-permute-done((f32[32,512]{1,0:T(8,128)S(1)}, f32[32,512]{1,0:T(8,128)S(1)}, u32[]{:S(2)}, u32[]{:S(2)}) %collective-permute-start.6) | collective-permute-done | bytes 65568 | tf_op jit(solution)/shard_map/ppermute | solution.py:196
  4.5 2.9 %collective-permute-start.7 = (f32[32,512]{1,0:T(8,128)S(1)}, f32[32,512]{1,0:T(8,128)S(1)}, u32[]{:S(2)}, u32[]{:S(2)}) collective-permute-start(f32[32,512]{1,0:T(8,128)S(1)} %add.35), channel_id=1, source_target_pairs={{0,1},{1,0},{2,3},{3,2},{4,5},{5,4},{6,7},{7,6},{8,9},{9,8},{10,11... | collective-permute-start | bytes 196616 | tf_op jit(solution)/shard_map/ppermute | solution.py:196
  7.4 0.0 collective-permute-done
  7.4 1.6 %collective-permute-start.1 = (f32[32,512]{1,0:T(8,128)S(1)}, f32[32,512]{1,0:T(8,128)S(1)}, u32[]{:S(2)}, u32[]{:S(2)}) collective-permute-start(f32[32,512]{1,0:T(8,128)S(1)} %add.30), channel_id=1, source_target_pairs={{0,2},{1,3},{2,0},{3,1},{4,6},{5,7},{6,4},{7,5},{8,10},{9,11},{10,... | collective-permute-start | bytes 196616 | tf_op jit(solution)/shard_map/ppermute | solution.py:196
  9.0 0.8 %collective-permute-done.7 = f32[32,512]{1,0:T(8,128)S(1)} collective-permute-done((f32[32,512]{1,0:T(8,128)S(1)}, f32[32,512]{1,0:T(8,128)S(1)}, u32[]{:S(2)}, u32[]{:S(2)}) %collective-permute-start.7) | collective-permute-done | bytes 65568 | tf_op jit(solution)/shard_map/ppermute | solution.py:196
  9.8 1.9 %collective-permute-start.8 = (f32[32,512]{1,0:T(8,128)S(1)}, f32[32,512]{1,0:T(8,128)S(1)}, u32[]{:S(2)}, u32[]{:S(2)}) collective-permute-start(f32[32,512]{1,0:T(8,128)S(1)} %add.36), channel_id=1, source_target_pairs={{0,16},{1,17},{2,18},{3,19},{4,20},{5,21},{6,22},{7,23},{8,24},{9,... | collective-permute-start | bytes 196616 | tf_op jit(solution)/shard_map/ppermute | solution.py:196
  11.7 0.0 collective-permute-done.1
  11.7 2.7 %collective-permute-start.2 = (f32[32,512]{1,0:T(8,128)S(1)}, f32[32,512]{1,0:T(8,128)S(1)}, u32[]{:S(2)}, u32[]{:S(2)}) collective-permute-start(f32[32,512]{1,0:T(8,128)S(1)} %add.31), channel_id=1, source_target_pairs={{0,4},{1,5},{2,6},{3,7},{4,0},{5,1},{6,2},{7,3},{8,12},{9,13},{10,... | collective-permute-start | bytes 196616 | tf_op jit(solution)/shard_map/ppermute | solution.py:196
  14.4 0.0 collective-permute-done.8
  14.4 1.7 %collective-permute-start.9 = (f32[32,512]{1,0:T(8,128)S(1)}, f32[32,512]{1,0:T(8,128)S(1)}, u32[]{:S(2)}, u32[]{:S(2)}) collective-permute-start(f32[32,512]{1,0:T(8,128)S(1)} %add.37), channel_id=1, source_target_pairs={{0,2},{1,3},{2,0},{3,1},{4,6},{5,7},{6,4},{7,5},{8,10},{9,11},{10,... | collective-permute-start | bytes 196616 | tf_op jit(solution)/shard_map/ppermute | solution.py:196
  16.1 0.8 %collective-permute-done.2 = f32[32,512]{1,0:T(8,128)S(1)} collective-permute-done((f32[32,512]{1,0:T(8,128)S(1)}, f32[32,512]{1,0:T(8,128)S(1)}, u32[]{:S(2)}, u32[]{:S(2)}) %collective-permute-start.2) | collective-permute-done | bytes 65568 | tf_op jit(solution)/shard_map/ppermute | solution.py:196
  17.0 1.6 %collective-permute-start.3 = (f32[32,512]{1,0:T(8,128)S(1)}, f32[32,512]{1,0:T(8,128)S(1)}, u32[]{:S(2)}, u32[]{:S(2)}) collective-permute-start(f32[32,512]{1,0:T(8,128)S(1)} %add.32), channel_id=1, source_target_pairs={{0,1},{1,0},{2,3},{3,2},{4,5},{5,4},{6,7},{7,6},{8,9},{9,8},{10,11... | collective-permute-start | bytes 196616 | tf_op jit(solution)/shard_map/ppermute | solution.py:196
  18.5 0.2 collective-permute-done.9
  18.8 2.7 %collective-permute-start.10 = (f32[32,512]{1,0:T(8,128)S(1)}, f32[32,512]{1,0:T(8,128)S(1)}, u32[]{:S(2)}, u32[]{:S(2)}) collective-permute-start(f32[32,512]{1,0:T(8,128)S(1)} %add.38), channel_id=1, source_target_pairs={{0,4},{1,5},{2,6},{3,7},{4,0},{5,1},{6,2},{7,3},{8,12},{9,13},{10,... | collective-permute-start | bytes 196616 | tf_op jit(solution)/shard_map/ppermute | solution.py:196
  21.5 0.0 collective-permute-done.3
  21.5 1.8 %collective-permute-start.4 = (f32[32,512]{1,0:T(8,128)S(1)}, f32[32,512]{1,0:T(8,128)S(1)}, u32[]{:S(2)}, u32[]{:S(2)}) collective-permute-start(f32[32,512]{1,0:T(8,128)S(1)} %add.33), channel_id=1, source_target_pairs={{0,16},{1,17},{2,18},{3,19},{4,20},{5,21},{6,22},{7,23},{8,24},{9,... | collective-permute-start | bytes 196616 | tf_op jit(solution)/shard_map/ppermute | solution.py:196
  23.3 0.7 %collective-permute-done.10 = f32[32,512]{1,0:T(8,128)S(1)} collective-permute-done((f32[32,512]{1,0:T(8,128)S(1)}, f32[32,512]{1,0:T(8,128)S(1)}, u32[]{:S(2)}, u32[]{:S(2)}) %collective-permute-start.10) | collective-permute-done | bytes 65568 | tf_op jit(solution)/shard_map/ppermute | solution.py:196
  24.0 0.1 collective-permute-start.11
  24.1 1.8 %collective-permute-done.4 = f32[32,512]{1,0:T(8,128)S(1)} collective-permute-done((f32[32,512]{1,0:T(8,128)S(1)}, f32[32,512]{1,0:T(8,128)S(1)}, u32[]{:S(2)}, u32[]{:S(2)}) %collective-permute-start.4) | collective-permute-done | bytes 65568 | tf_op jit(solution)/shard_map/ppermute | solution.py:196
  25.9 0.1 collective-permute-start.5
  25.9 0.0 collective-permute-done.11.other
  25.9 0.4 %blocks.1 = (bf16[64,256]{1,0:T(8,128)(2,1)S(1)}, bf16[192,256]{1,0:T(8,128)(2,1)S(1)}, f32[64,128]{1,0:T(8,128)S(1)}, f32[64,384]{1,0:T(8,128)S(1)}) custom-call(f32[32,512]{1,0:T(8,128)S(1)} %add.39.mine, f32[32,512]{1,0:T(8,128)S(1)} %collective-permute-done.11.other, bf16[256,256]{1,0:T(8,128)(2,1)S(1)} %get-tuple-element.22.points_ref, ...), custom_call_target="tpu_custom_call" | custom-call | flops 10000000 | bytes 524288 | tf_op jit(solution)/shard_map/blocks/pallas_call | solution.py:244
  26.3 1.3 %first.1 = (bf16[64,384]{1,0:T(8,128)(2,1)S(1)}, f32[64,256]{1,0:T(8,128)S(1)}) custom-call(f32[64,384]{1,0:T(8,128)S(1)} %get-tuple-element.33.work_ref), custom_call_target="tpu_custom_call" | custom-call | flops 10000000 | bytes 524288 | tf_op jit(solution)/shard_map/first/pallas_call | solution.py:259
  27.6 0.0 collective-permute-done.5.other
  27.6 2.6 %second.1 = (f32[256,128]{1,0:T(8,128)}, f32[1,256]{1,0:T(1,128)}) custom-call(f32[32,512]{1,0:T(8,128)S(1)} %add.34.mine, f32[32,512]{1,0:T(8,128)S(1)} %collective-permute-done.5.other, bf16[256,256]{1,0:T(8,128)(2,1)S(1)} %get-tuple-element.22.points_ref, bf16[256,256]{1,0:T(8,128)(2,1)S(1)} %get-tuple-element.23.high_ref, ...), custom_call_target="tpu_custom_call" | custom-call | tf_op jit(solution)/shard_map/second/pallas_call | solution.py:268
  (10 shorter events, 0.1 us)
Async XLA Ops:
  0.6 0.7 %copy-start = (s32[2,64]{1,0:T(2,128)S(1)}, s32[2,64]{1,0:T(2,128)}, u32[]{:S(2)}) copy-start(s32[2,64]{1,0:T(2,128)} %pivots_ref.1) | copy-start | bytes 1540
  3.0 1.5 %collective-permute-start.6 = (f32[32,512]{1,0:T(8,128)S(1)}, f32[32,512]{1,0:T(8,128)S(1)}, u32[]{:S(2)}, u32[]{:S(2)}) collective-permute-start(f32[32,512]{1,0:T(8,128)S(1)} %get-tuple-element.29), channel_id=1, source_target_pairs={{0,8},{1,9},{2,10},{3,11},{4,12},{5,13},{6,14},{7,15},{8,0},{9,1},... | collective-permute-start | bytes 196616 | tf_op jit(solution)/shard_map/ppermute | solution.py:196
  3.5 3.8 %collective-permute-start = (f32[32,512]{1,0:T(8,128)S(1)}, f32[32,512]{1,0:T(8,128)S(1)}, u32[]{:S(2)}, u32[]{:S(2)}) collective-permute-start(f32[32,512]{1,0:T(8,128)S(1)} %get-tuple-element.21), channel_id=1, source_target_pairs={{0,8},{1,9},{2,10},{3,11},{4,12},{5,13},{6,14},{7,15},{8,0},{9,1},... | collective-permute-start | bytes 196616 | tf_op jit(solution)/shard_map/ppermute | solution.py:196
  4.5 5.3 %collective-permute-start.7 = (f32[32,512]{1,0:T(8,128)S(1)}, f32[32,512]{1,0:T(8,128)S(1)}, u32[]{:S(2)}, u32[]{:S(2)}) collective-permute-start(f32[32,512]{1,0:T(8,128)S(1)} %add.35), channel_id=1, source_target_pairs={{0,1},{1,0},{2,3},{3,2},{4,5},{5,4},{6,7},{7,6},{8,9},{9,8},{10,11... | collective-permute-start | bytes 196616 | tf_op jit(solution)/shard_map/ppermute | solution.py:196
  7.4 4.4 %collective-permute-start.1 = (f32[32,512]{1,0:T(8,128)S(1)}, f32[32,512]{1,0:T(8,128)S(1)}, u32[]{:S(2)}, u32[]{:S(2)}) collective-permute-start(f32[32,512]{1,0:T(8,128)S(1)} %add.30), channel_id=1, source_target_pairs={{0,2},{1,3},{2,0},{3,1},{4,6},{5,7},{6,4},{7,5},{8,10},{9,11},{10,... | collective-permute-start | bytes 196616 | tf_op jit(solution)/shard_map/ppermute | solution.py:196
  9.8 4.6 %collective-permute-start.8 = (f32[32,512]{1,0:T(8,128)S(1)}, f32[32,512]{1,0:T(8,128)S(1)}, u32[]{:S(2)}, u32[]{:S(2)}) collective-permute-start(f32[32,512]{1,0:T(8,128)S(1)} %add.36), channel_id=1, source_target_pairs={{0,16},{1,17},{2,18},{3,19},{4,20},{5,21},{6,22},{7,23},{8,24},{9,... | collective-permute-start | bytes 196616 | tf_op jit(solution)/shard_map/ppermute | solution.py:196
  11.7 5.2 %collective-permute-start.2 = (f32[32,512]{1,0:T(8,128)S(1)}, f32[32,512]{1,0:T(8,128)S(1)}, u32[]{:S(2)}, u32[]{:S(2)}) collective-permute-start(f32[32,512]{1,0:T(8,128)S(1)} %add.31), channel_id=1, source_target_pairs={{0,4},{1,5},{2,6},{3,7},{4,0},{5,1},{6,2},{7,3},{8,12},{9,13},{10,... | collective-permute-start | bytes 196616 | tf_op jit(solution)/shard_map/ppermute | solution.py:196
  14.4 4.3 %collective-permute-start.9 = (f32[32,512]{1,0:T(8,128)S(1)}, f32[32,512]{1,0:T(8,128)S(1)}, u32[]{:S(2)}, u32[]{:S(2)}) collective-permute-start(f32[32,512]{1,0:T(8,128)S(1)} %add.37), channel_id=1, source_target_pairs={{0,2},{1,3},{2,0},{3,1},{4,6},{5,7},{6,4},{7,5},{8,10},{9,11},{10,... | collective-permute-start | bytes 196616 | tf_op jit(solution)/shard_map/ppermute | solution.py:196
  17.0 4.5 %collective-permute-start.3 = (f32[32,512]{1,0:T(8,128)S(1)}, f32[32,512]{1,0:T(8,128)S(1)}, u32[]{:S(2)}, u32[]{:S(2)}) collective-permute-start(f32[32,512]{1,0:T(8,128)S(1)} %add.32), channel_id=1, source_target_pairs={{0,1},{1,0},{2,3},{3,2},{4,5},{5,4},{6,7},{7,6},{8,9},{9,8},{10,11... | collective-permute-start | bytes 196616 | tf_op jit(solution)/shard_map/ppermute | solution.py:196
  18.8 5.2 %collective-permute-start.10 = (f32[32,512]{1,0:T(8,128)S(1)}, f32[32,512]{1,0:T(8,128)S(1)}, u32[]{:S(2)}, u32[]{:S(2)}) collective-permute-start(f32[32,512]{1,0:T(8,128)S(1)} %add.38), channel_id=1, source_target_pairs={{0,4},{1,5},{2,6},{3,7},{4,0},{5,1},{6,2},{7,3},{8,12},{9,13},{10,... | collective-permute-start | bytes 196616 | tf_op jit(solution)/shard_map/ppermute | solution.py:196
  21.5 4.3 %collective-permute-start.4 = (f32[32,512]{1,0:T(8,128)S(1)}, f32[32,512]{1,0:T(8,128)S(1)}, u32[]{:S(2)}, u32[]{:S(2)}) collective-permute-start(f32[32,512]{1,0:T(8,128)S(1)} %add.33), channel_id=1, source_target_pairs={{0,16},{1,17},{2,18},{3,19},{4,20},{5,21},{6,22},{7,23},{8,24},{9,... | collective-permute-start | bytes 196616 | tf_op jit(solution)/shard_map/ppermute | solution.py:196
  24.0 1.9 %collective-permute-start.11 = (f32[32,512]{1,0:T(8,128)S(1)}, f32[32,512]{1,0:T(8,128)S(1)}, u32[]{:S(2)}, u32[]{:S(2)}) collective-permute-start(f32[32,512]{1,0:T(8,128)S(1)} %add.39.mine), channel_id=1, source_target_pairs={{0,8},{1,9},{2,10},{3,11},{4,12},{5,13},{6,14},{7,15},{8,0},{9,1},... | collective-permute-start | bytes 196616 | tf_op jit(solution)/shard_map/ppermute | solution.py:196
  25.9 1.7 %collective-permute-start.5 = (f32[32,512]{1,0:T(8,128)S(1)}, f32[32,512]{1,0:T(8,128)S(1)}, u32[]{:S(2)}, u32[]{:S(2)}) collective-permute-start(f32[32,512]{1,0:T(8,128)S(1)} %add.34.mine), channel_id=1, source_target_pairs={{0,8},{1,9},{2,10},{3,11},{4,12},{5,13},{6,14},{7,15},{8,0},{9,1},... | collective-permute-start | bytes 196616 | tf_op jit(solution)/shard_map/ppermute | solution.py:196
